TPU v7x, 32 devices: a whole 2x2x4 slice. The times are simulated.
32 devices in a mesh: py: 4 (over y, core), pz: 8 (over z, x).
Axes of the slice: x: 2, y: 2, z: 4, core: 2. Of those that a mesh axis runs over, the one named last changes fastest.
Arguments:
- wavefunctions: float32 [2, 8, 128, 128, 128], P(None, None, 'pz', 'py'), may hold values from -6 to 6
- potential: float32 [128, 128, 128], P('pz', 'py'), may hold values from -4 to 4
- cutoff_sq: int32 [1], replicated, may hold values from 2304 to 4096
- locked_mask: int32 [8], replicated, may hold values 0 or 1
Outputs:
- applied: float32 [2, 8, 128, 128, 128], P(None, None, 'pz', 'py')
- rayleigh: float32 [8], replicated
- residual_norm: float32 [8], replicated
All inputs are finite; a program needn't handle non-finite values.
Results may differ from a plain program's by a relative error of at most 0.00005.
Values sent between devices are 32-bit elements; how exact they have to be, the bound alone decides.
A program may use at most 64 MiB of HBM per device.

v0:
```python
import functools
import math

import jax
import jax.numpy as jnp
import numpy as np
from jax import lax
from jax.experimental import pallas as pl
from jax.experimental.pallas import tpu as pltpu
from jax.sharding import PartitionSpec as P

PREC = lax.Precision.HIGHEST
MESH = pl.DeviceIdType.MESH


def make_tables(length, inverse):
    counter = jnp.arange(length, dtype=jnp.int32)
    phase = counter[:, None] * counter[None, :] % length
    angle = 2.0 * math.pi / length * phase.astype(jnp.float32)
    if inverse:
        return (jnp.cos(angle) / length, jnp.sin(angle) / length)
    return (jnp.cos(angle), -jnp.sin(angle))


def transform(form, pair, tables):
    re, im = pair
    cosines, sines = tables

    def dot(field, table):
        return jnp.einsum(form, field, table, precision=PREC)

    return (dot(re, cosines) - dot(im, sines), dot(re, sines) + dot(im, cosines))


def exchange(pair, axis, split, concat):
    return tuple(
        lax.all_to_all(part, axis, split_axis=split, concat_axis=concat, tiled=True)
        for part in pair
    )


def signed_square(counter, length):
    signed = jnp.where(counter < length // 2, counter, counter - length)
    return signed * signed


def right_matrix(tables):
    cosines, sines = tables
    top = jnp.concatenate([cosines, sines], axis=1)
    return jnp.concatenate([top, jnp.concatenate([-sines, cosines], axis=1)], axis=0)


def fold_rows(length, extra):
    half = length // 2
    reach = {f: math.isqrt(half * half - f * f) for f in range(-half, half)}
    guests = [f for f in sorted(reach, key=lambda f: (reach[f], f)) if f != -half][:extra]
    free = [f for f in reach if f not in guests and f != -half]
    hosts = []
    for g in reversed(guests):
        fits = [f for f in free if reach[f] + reach[g] < half]
        if not fits:
            return None
        hosts.append(min(fits, key=lambda f: (abs(f), f)))
        free.remove(hosts[-1])
    hosts = hosts[::-1]
    plain = [f for f in sorted(reach) if f not in hosts and f not in guests]
    order = np.array(plain + hosts + guests)
    lanes = np.arange(length)
    signed = np.where(lanes < half, lanes, lanes - length)
    moved = np.roll(signed, half)
    mask = np.abs(signed)[None, :] <= np.array([reach[f] for f in hosts])[:, None]
    hosts, guests = np.array(hosts), np.array(guests)
    square = np.concatenate([
        np.array(plain)[:, None] ** 2 + signed[None, :] ** 2,
        np.where(mask, hosts[:, None] ** 2 + signed[None, :] ** 2,
                 guests[:, None] ** 2 + moved[None, :] ** 2)])
    return order % length, mask.astype(np.float32), square.astype(np.int32)


def dot(left, right):
    return jnp.dot(left, right, precision=PREC, preferred_element_type=jnp.float32)


def main_kernel(
    size_y, size_z, chunks,
    u_ref, kin_ref, xf_ref, xi_ref, lf_ref, li_ref, yf_ref, yi_ref, mask_ref, out_ref,
    a1, r1, a2, r2, r3,
    s1, q1, s2, q2, s3, q3, s4, q4,
):
    me_y, me_z = lax.axis_index("py"), lax.axis_index("pz")
    _, bands, rows_z, rows_y, length = u_ref.shape
    slots = bands // size_y
    rows_k = kin_ref.shape[0]
    extra = mask_ref.shape[0]
    hosts = length - 2 * extra
    step = rows_z // chunks
    high = length

    barrier = pltpu.get_barrier_semaphore()
    for d in range(1, size_y):
        pl.semaphore_signal(barrier, inc=1, device_id={"py": (me_y + d) % size_y}, device_id_type=MESH)
    for d in range(1, size_z):
        pl.semaphore_signal(barrier, inc=1, device_id={"pz": (me_z + d) % size_z}, device_id_type=MESH)
    pl.semaphore_wait(barrier, size_y + size_z - 2)

    def copy1(s, c, d):
        to = (me_y + d) % size_y
        return pltpu.make_async_remote_copy(
            src_ref=a1.at[:, to * slots + s, pl.ds(c * step, step)],
            dst_ref=r1.at[:, s, pl.ds(c * step, step), me_y],
            send_sem=s1.at[s, c, d - 1], recv_sem=q1.at[s, c, d - 1],
            device_id={"py": to}, device_id_type=MESH)

    def copy2(s, c, d):
        to = (me_z + d) % size_z
        rows = step * rows_k
        return pltpu.make_async_remote_copy(
            src_ref=a2.at[:, s, to, pl.ds(pl.multiple_of(c * rows, rows), rows)],
            dst_ref=r2.at[:, s, pl.ds(pl.multiple_of((me_z * chunks + c) * rows, rows), rows)],
            send_sem=s2.at[s, c, d - 1], recv_sem=q2.at[s, c, d - 1],
            device_id={"pz": to}, device_id_type=MESH)

    def copy3(s, c, d):
        to = (me_z + d) % size_z
        rows = step * rows_k
        return pltpu.make_async_remote_copy(
            src_ref=r2.at[:, s, pl.ds(pl.multiple_of((to * chunks + c) * rows, rows), rows)],
            dst_ref=r3.at[:, s, me_z, pl.ds(pl.multiple_of(c * rows, rows), rows)],
            send_sem=s3.at[s, c, d - 1], recv_sem=q3.at[s, c, d - 1],
            device_id={"pz": to}, device_id_type=MESH)

    def copy4(s, c, d):
        to = (me_y + d) % size_y
        return pltpu.make_async_remote_copy(
            src_ref=r1.at[:, s, pl.ds(c * step, step), to],
            dst_ref=out_ref.at[:, me_y * slots + s, pl.ds(c * step, step)],
            send_sem=s4.at[s, c, d - 1], recv_sem=q4.at[s, c, d - 1],
            device_id={"py": to}, device_id_type=MESH)

    order_z = sorted(range(1, size_z), key=lambda d: -min(d, size_z - d))

    for s in range(slots):
        def forward_x(c, carry):
            for d in list(range(1, size_y)) + [0]:
                band = (me_y + d) % size_y * slots + s
                zs = pl.ds(c * step, step)
                rows = jnp.concatenate(
                    [u_ref[p, band, zs].reshape(step * rows_y, length) for p in range(2)], axis=1)
                done = dot(rows, xf_ref[...])
                for p in range(2):
                    part = done[:, p * high : (p + 1) * high].reshape(step, rows_y, length)
                    if d == 0:
                        r1[p, s, zs, me_y] = part
                    else:
                        a1[p, band, zs] = part
                if d > 0:
                    copy1(s, c, d).start()
            return carry
        lax.fori_loop(0, chunks, forward_x, 0)

    for s in range(slots):
        def forward_y(c, carry):
            for d in range(1, size_y):
                copy1(s, c, d).wait_recv()
            folded = [[], []]
            for i in range(0, step, 2):
                sides = []
                for z in (c * step + i, c * step + i + 1):
                    sides.append(jnp.concatenate(
                        [r1[p, s, z].reshape(length, length) for p in range(2)], axis=0))
                done = dot(yf_ref[...], jnp.concatenate(sides, axis=1))
                for p in range(2):
                    for e in range(2):
                        part = done[p * high : (p + 1) * high, e * high : (e + 1) * high]
                        mask = mask_ref[...]
                        guest = pltpu.roll(part[hosts + extra :], length // 2, axis=1)
                        shared = part[hosts : hosts + extra] * mask + guest * (1.0 - mask)
                        folded[p].append(jnp.concatenate([part[:hosts], shared], axis=0))
            rows = step * rows_k
            at = pl.ds(pl.multiple_of(c * rows, rows), rows)
            for p in range(2):
                for m in range(size_z):
                    a2[p, s, m, at] = jnp.concatenate(
                        [part[m * rows_k : (m + 1) * rows_k] for part in folded[p]], axis=0)
            for d in order_z:
                copy2(s, c, d).start()
            rows = step * rows_k
            own = pl.ds(pl.multiple_of(c * rows, rows), rows)
            r2[:, s, pl.ds(pl.multiple_of((me_z * chunks + c) * rows, rows), rows)] = a2[:, s, me_z, own]
            return carry
        lax.fori_loop(0, chunks, forward_y, 0)

    for s in range(slots):
        def arrive2(c, carry):
            for d in range(1, size_z):
                copy2(s, c, d).wait_recv()
            return carry
        lax.fori_loop(0, chunks, arrive2, 0)

        def both_z(h, carry):
            sides = []
            for k in (2 * h, 2 * h + 1):
                sides.append(jnp.concatenate(
                    [r2[p, s, pl.ds(k, length, stride=rows_k)] for p in range(2)], axis=0))
            spectrum = dot(lf_ref[...], jnp.concatenate(sides, axis=1))
            weight = jnp.concatenate([kin_ref[2 * h], kin_ref[2 * h + 1]], axis=1)
            weight = jnp.concatenate([weight, weight], axis=0)
            done = dot(li_ref[...], spectrum * weight)
            for p in range(2):
                for e in range(2):
                    r2[p, s, pl.ds(2 * h + e, length, stride=rows_k)] = done[
                        p * high : (p + 1) * high, e * high : (e + 1) * high]
            return carry
        lax.fori_loop(0, rows_k // 2, both_z, 0)

        def leave3(c, carry):
            for d in order_z:
                copy3(s, c, d).start()
            return carry
        lax.fori_loop(0, chunks, leave3, 0)
        every = rows_z * rows_k
        r3[:, s, me_z] = r2[:, s, pl.ds(pl.multiple_of(me_z * every, every), every)]

    for s in range(slots):
        def inverse_y(c, carry):
            for d in range(1, size_z):
                copy3(s, c, d).wait_recv()
            rows = step * rows_k
            at = pl.ds(pl.multiple_of(c * rows, rows), rows)
            held = [[r3[p, s, m, at] for m in range(size_z)] for p in range(2)]
            for i in range(0, step, 2):
                sides = []
                for e in range(2):
                    both = []
                    for p in range(2):
                        part = jnp.concatenate(
                            [held[p][m][(i + e) * rows_k : (i + e + 1) * rows_k]
                             for m in range(size_z)], axis=0)
                        mask = mask_ref[...]
                        shared = part[hosts:]
                        guest = pltpu.roll(shared * (1.0 - mask), length // 2, axis=1)
                        both += [part[:hosts], shared * mask, guest]
                    sides.append(jnp.concatenate(both, axis=0))
                done = dot(yi_ref[...], jnp.concatenate(sides, axis=1))
                for p in range(2):
                    for e in range(2):
                        part = done[p * high : (p + 1) * high, e * high : (e + 1) * high]
                        r1[p, s, c * step + i + e] = part.reshape(size_y, rows_y, length)
            for d in range(1, size_y):
                copy4(s, c, d).start()
            zs = pl.ds(c * step, step)
            out_ref[:, me_y * slots + s, zs] = r1[:, s, zs, me_y]
            return carry
        lax.fori_loop(0, chunks, inverse_y, 0)

    for s in range(slots):
        def inverse_x(c, carry):
            zs = pl.ds(c * step, step)
            for d in range(size_y):
                band = (me_y + size_y - d) % size_y * slots + s
                if d > 0:
                    copy4(s, c, d).wait_recv()
                rows = jnp.concatenate(
                    [out_ref[p, band, zs].reshape(step * rows_y, length) for p in range(2)], axis=1)
                done = dot(rows, xi_ref[...])
                for p in range(2):
                    out_ref[p, band, zs] = done[:, p * high : (p + 1) * high].reshape(
                        step, rows_y, length)
            return carry
        lax.fori_loop(0, chunks, inverse_x, 0)

    for s in range(slots):
        def settle(c, carry):
            for d in range(1, size_y):
                copy1(s, c, d).wait_send()
                copy4(s, c, d).wait_send()
            for d in range(1, size_z):
                copy2(s, c, d).wait_send()
                copy3(s, c, d).wait_send()
            return carry
        lax.fori_loop(0, chunks, settle, 0)


def fused_kinetic(wavefunctions, cutoff_sq, folding, forward, inverse):
    order, mask, square = folding
    _, bands, rows_z, rows_y, length = wavefunctions.shape
    size_y, size_z = lax.axis_size("py"), lax.axis_size("pz")
    slots = bands // size_y
    rows_k = square.shape[0] // size_z
    chunks = rows_z // 4
    xf, xi = right_matrix(forward), right_matrix(inverse)
    both = np.concatenate([order, order + length])
    own_sq = lax.dynamic_slice_in_dim(jnp.asarray(square), lax.axis_index("pz") * rows_k, rows_k, 0)
    full_sq = signed_square(jnp.arange(length, dtype=jnp.int32), length)
    kinetic = weigh(own_sq[:, None, :] + full_sq[None, :, None], cutoff_sq, length)
    tables = (kinetic, xf, xi, xf.T, xi.T, xf.T[both], xi.T[:, both], jnp.asarray(mask))
    vmem = pl.BlockSpec(memory_space=pltpu.VMEM)
    near = pltpu.SemaphoreType.DMA((slots, chunks, size_y - 1))
    far = pltpu.SemaphoreType.DMA((slots, chunks, size_z - 1))
    return pl.pallas_call(
        functools.partial(main_kernel, size_y, size_z, chunks),
        out_shape=jax.ShapeDtypeStruct(wavefunctions.shape, jnp.float32),
        in_specs=[vmem] * 9,
        out_specs=vmem,
        scratch_shapes=[
            pltpu.VMEM((2, bands, rows_z, rows_y, length), jnp.float32),
            pltpu.VMEM((2, slots, rows_z, size_y, rows_y, length), jnp.float32),
            pltpu.VMEM((2, slots, size_z, rows_z * rows_k, length), jnp.float32),
            pltpu.VMEM((2, slots, length * rows_k, length), jnp.float32),
            pltpu.VMEM((2, slots, size_z, rows_z * rows_k, length), jnp.float32),
            near, near, far, far, far, far, near, near,
        ],
        compiler_params=pltpu.CompilerParams(
            collective_id=0, has_side_effects=True, vmem_limit_bytes=67043328),
    )(wavefunctions, *tables)


def gather_kernel(size_y, size_z, own_ref, out_ref, send, recv):
    me_y, me_z = lax.axis_index("py"), lax.axis_index("pz")
    me = me_y * size_z + me_z
    count = size_y * size_z
    barrier = pltpu.get_barrier_semaphore()

    def target(t):
        to = (me + t) % count
        return {"py": to // size_z, "pz": to % size_z}

    def greet(t, carry):
        pl.semaphore_signal(barrier, inc=1, device_id=target(t), device_id_type=MESH)
        return carry
    lax.fori_loop(1, count, greet, 0)
    pl.semaphore_wait(barrier, count - 1)

    def copy(t):
        return pltpu.make_async_remote_copy(
            src_ref=own_ref, dst_ref=out_ref.at[me], send_sem=send.at[t], recv_sem=recv.at[t],
            device_id=target(t), device_id_type=MESH)

    def leave(t, carry):
        copy(t).start()
        return carry
    lax.fori_loop(1, count, leave, 0)
    out_ref[me] = own_ref[...]

    def arrive(t, carry):
        copy(t).wait()
        return carry
    lax.fori_loop(1, count, arrive, 0)


def gather_sums(sums):
    size_y, size_z = lax.axis_size("py"), lax.axis_size("pz")
    count = size_y * size_z
    kinds, bands = sums.shape
    if count > 64:
        return lax.all_gather(sums, ("py", "pz"))
    own = jnp.pad(sums, ((0, 8 - kinds), (0, 128 - bands)))
    vmem = pl.BlockSpec(memory_space=pltpu.VMEM)
    every = pl.pallas_call(
        functools.partial(gather_kernel, size_y, size_z),
        out_shape=jax.ShapeDtypeStruct((count, 8, 128), jnp.float32),
        in_specs=[vmem],
        out_specs=vmem,
        scratch_shapes=[pltpu.SemaphoreType.DMA((count,)), pltpu.SemaphoreType.DMA((count,))],
        compiler_params=pltpu.CompilerParams(collective_id=1, has_side_effects=True),
    )(own)
    return every[:, :kinds, :bands]


def weigh(total, cutoff_sq, length):
    keep = (total <= cutoff_sq[0]).astype(jnp.float32)
    return 0.5 * (math.pi / length) ** 2 * total.astype(jnp.float32) * keep


def plain_kinetic(wavefunctions, kinetic, forward, inverse):
    along_x = "bzyn,kn->bzyk"
    along_y = "bznx,kn->bzkx"
    along_z = "bnyx,kn->bkyx"
    pair = (wavefunctions[0], wavefunctions[1])
    pair = transform(along_x, pair, forward)
    pair = exchange(pair, "py", 0, 2)
    pair = transform(along_y, pair, forward)
    pair = exchange(pair, "pz", 2, 1)
    pair = transform(along_z, pair, forward)
    pair = tuple(part * jnp.swapaxes(kinetic, 0, 1)[None] for part in pair)
    pair = transform(along_z, pair, inverse)
    pair = exchange(pair, "pz", 1, 2)
    pair = transform(along_y, pair, inverse)
    pair = exchange(pair, "py", 2, 0)
    pair = transform(along_x, pair, inverse)
    return jnp.stack(pair)


def body(wavefunctions, potential, cutoff_sq, locked_mask):
    length = wavefunctions.shape[4]
    forward = make_tables(length, False)
    inverse = make_tables(length, True)
    size_y, size_z = lax.axis_size("py"), lax.axis_size("pz")
    rows = length // size_z
    extra = 2 * size_z
    kept = rows - 2
    fits = extra % 8 == 0 and 4 * kept % 8 == 0 and kept > 2 and rows % 8 == 0
    fits = fits and wavefunctions.shape[2] % 4 == 0 and wavefunctions.shape[1] % size_y == 0
    folding = fold_rows(length, extra) if fits else None
    if folding is not None:
        back = fused_kinetic(wavefunctions, cutoff_sq, folding, forward, inverse)
    else:
        full_sq = signed_square(jnp.arange(length, dtype=jnp.int32), length)
        own = lax.axis_index("pz") * rows + jnp.arange(rows, dtype=jnp.int32)
        own_sq = signed_square(own, length)
        total = own_sq[:, None, None] + full_sq[None, :, None] + full_sq[None, None, :]
        kinetic = weigh(total, cutoff_sq, length)
        back = plain_kinetic(wavefunctions, kinetic, forward, inverse)
    applied = back + potential[None, None] * wavefunctions
    norm_own = jnp.sum(wavefunctions * wavefunctions, axis=(0, 2, 3, 4))
    corr_own = jnp.sum(wavefunctions * applied, axis=(0, 2, 3, 4))
    shift = jnp.where(norm_own > 0.0, corr_own / jnp.where(norm_own > 0.0, norm_own, 1.0), 0.0)
    rest = applied - shift[None, :, None, None, None] * wavefunctions
    rest_sq = jnp.sum(rest * rest, axis=(0, 2, 3, 4))
    rest_dot = jnp.sum(rest * wavefunctions, axis=(0, 2, 3, 4))
    sums = jnp.stack([norm_own, corr_own, shift, rest_sq, rest_dot])
    every = gather_sums(sums)
    norm_all, corr_all, shift_all, sq_all, dot_all = (every[:, i] for i in range(5))
    norm_sq = jnp.sum(norm_all, axis=0)
    rayleigh = jnp.sum(corr_all, axis=0) / norm_sq
    gap = shift_all - rayleigh[None]
    residual_sq = jnp.sum(sq_all + 2.0 * gap * dot_all + gap * gap * norm_all, axis=0)
    residual_sq = jnp.maximum(residual_sq, 0.0)
    residual_norm = jnp.sqrt(residual_sq / norm_sq) * (1.0 - locked_mask.astype(jnp.float32))
    return (applied, rayleigh, residual_norm)


def solution(mesh):
    in_specs = (P(None, None, "pz", "py", None), P("pz", "py", None), P(), P())
    out_specs = (P(None, None, "pz", "py", None), P(), P())
    return jax.shard_map(body, mesh=mesh, in_specs=in_specs, out_specs=out_specs, check_vma=False)
```

profile of v0, /device:TPU:0, one launch (start us, length us, event | category | flops | bytes accessed | tf_op | source)
XLA Modules:
  0.0 226.7 jit_solution(1218377258146025458)
XLA Ops:
  1.3 0.7 pad_clamp_fusion
  2.0 0.7 constant_dynamic-slice_fusion
  2.7 0.3 fusion.11
  3.0 0.3 fusion.10
  3.2 0.3 fusion.8
  3.5 0.3 broadcast_multiply_fusion
  3.8 0.0 copy-start.3
  3.8 0.8 copy.15.xi_ref
  4.7 0.1 copy.12
  4.8 1.0 gather_fusion.1
  5.8 0.9 copy.13
  6.7 0.0 copy-start.1
  6.7 0.8 copy.14.xf_ref
  7.5 0.0 copy-done.1
  7.5 1.7 gather_fusion
  9.2 0.0 copy-done.3
  9.2 1.1 fusion.1.kin_ref
  10.3 195.4 %shard_map.112 = f32[2,8,16,32,128]{4,3,2,1,0:T(8,128)} custom-call(f32[2,8,16,32,128]{4,3,2,1,0:T(8,128)} %u_ref.1, f32[14,128,128]{2,1,0:T(8,128)} %fusion.1.kin_ref, f32[256,256]{1,0:T(8,128)} %copy.14.xf_ref, f32[256,256]{1,0:T(8,128)} %copy.15.xi_ref, f32[256,256]{1,0:T(8,128)} %copy-done.1, f32[256,256]{1,0:T(8,128)} %copy-done.3, ...), custom_call_target="tpu_custom_call" | custom-call | tf_op jit(solution)/shard_map/pallas_call | solution.py:300
  205.7 0.0 copy-start
  205.7 5.3 %multiply_reduce_fusion.2 = (f32[8]{0:T(128)S(1)}, f32[8]{0:T(128)S(1)}, f32[2,8,16,32,128]{4,3,2,1,0:T(8,128)S(1)}) fusion(f32[2,8,16,32,128]{4,3,2,1,0:T(8,128)} %u_ref.1, f32[2,8,16,32,128]{4,3,2,1,0:T(8,128)} %shard_map.112, f32[16,32,128]{2,1,0:T(8,128)} %param.10), kind=kLoop, calls=%fused_computation.5 | loop fusion | flops 6291440 | bytes 12845120 | tf_op jit(solution)/shard_map/reduce_sum | solution.py:416
  211.0 0.0 copy-start.2
  211.0 0.0 copy-done
  211.1 0.0 copy-start.5
  211.1 1.6 multiply_reduce_fusion
  212.7 0.4 copy-done.2
  213.1 0.6 pad.4.own_ref
  213.6 11.2 %shard_map.113 = f32[32,8,128]{2,1,0:T(8,128)} custom-call(f32[8,128]{1,0:T(8,128)} %pad.4.own_ref), custom_call_target="tpu_custom_call" | custom-call | tf_op jit(solution)/shard_map/pallas_call | solution.py:359
  224.8 1.3 fusion.17
  226.1 0.0 copy-start.4
  226.2 0.0 copy-done.5
  226.2 0.5 subtract_multiply_fusion
  226.7 0.0 copy-done.4
  (9 shorter events, 0.2 us)
Async XLA Ops:
  3.8 5.4 %copy-start.3 = (f32[256,256]{1,0:T(8,128)}, f32[256,256]{1,0:T(8,128)S(1)}, u32[]{:S(2)}) copy-start(f32[256,256]{1,0:T(8,128)S(1)} %get-tuple-element.8.li_ref) | copy-start | bytes 786436
  6.7 0.8 copy-start.1
  205.7 5.3 %copy-start = (f32[2,8,16,32,128]{4,3,2,1,0:T(8,128)S(1)}, f32[2,8,16,32,128]{4,3,2,1,0:T(8,128)}, u32[]{:S(2)}) copy-start(f32[2,8,16,32,128]{4,3,2,1,0:T(8,128)} %u_ref.1) | copy-start | bytes 12582916
  211.0 2.0 copy-start.2
  211.1 15.1 %copy-start.5 = (s32[8]{0:T(128)S(1)}, s32[8]{0:T(128)}, u32[]{:S(2)}) copy-start(s32[8]{0:T(128)} %param.12) | copy-start | bytes 100
  226.1 0.6 copy-start.4
where the time goes:
time: 227 us
  Pallas kernels  207 us (91%)
  other arithmetic  11.8 us (5%)
  local copies, waits for them, and re-layouts  6.99 us (3%)
    pallas_call x1, Pallas kernels, fused_kinetic(): pl.pallas_call(functools.partial(main_kernel, size_y, size_z, chunks), ou...  195 us
    pallas_call x1, Pallas kernels, gather_sums(): pl.pallas_call(functools.partial(gather_kernel, size_y, size_z), out_shap...  11.2 us
    reduce_sum x1, other arithmetic, body(): corr_own = jnp.sum(wavefunctions * applied, axis=(0, 2, 3, 4))  5.29 us

commit v1 on v0

v1 whole, which is shorter than its diff:
```python
import functools
import math

import jax
import jax.numpy as jnp
import numpy as np
from jax import lax
from jax.experimental import pallas as pl
from jax.experimental.pallas import tpu as pltpu
from jax.sharding import PartitionSpec as P

PREC = lax.Precision.HIGHEST
MESH = pl.DeviceIdType.MESH


def make_tables(length, inverse):
    counter = jnp.arange(length, dtype=jnp.int32)
    phase = counter[:, None] * counter[None, :] % length
    angle = 2.0 * math.pi / length * phase.astype(jnp.float32)
    if inverse:
        return (jnp.cos(angle) / length, jnp.sin(angle) / length)
    return (jnp.cos(angle), -jnp.sin(angle))


def transform(form, pair, tables):
    re, im = pair
    cosines, sines = tables

    def dot(field, table):
        return jnp.einsum(form, field, table, precision=PREC)

    return (dot(re, cosines) - dot(im, sines), dot(re, sines) + dot(im, cosines))


def exchange(pair, axis, split, concat):
    return tuple(
        lax.all_to_all(part, axis, split_axis=split, concat_axis=concat, tiled=True)
        for part in pair
    )


def signed_square(counter, length):
    signed = jnp.where(counter < length // 2, counter, counter - length)
    return signed * signed


def right_matrix(tables):
    cosines, sines = tables
    top = jnp.concatenate([cosines, sines], axis=1)
    return jnp.concatenate([top, jnp.concatenate([-sines, cosines], axis=1)], axis=0)


def fold_rows(length, lanes_of, extra):
    half = length // 2
    group = lanes_of
    reach = {f: math.isqrt(half * half - f * f) for f in range(-half, half)}
    pairs = group // 2
    first_guest = half - extra // 2
    guests = [list(range(first_guest + i, first_guest + i + pairs)) for i in range(0, extra // 2, pairs)]
    hosts = []
    top = first_guest
    while top - pairs > 0 and length - 1 - 2 * reach[top - 1] > 2 and len(hosts) < 8:
        hosts.append(list(range(top - 1, top - 1 - pairs, -1)))
        top -= pairs
    taken = {f for rows in guests + hosts for f in rows}
    plain = [f for f in range(-half, half) if abs(f) not in taken]
    if len(plain) % group or not hosts:
        return None
    hosts = hosts[::-1]
    first = len(plain) // group
    lanes = np.arange(length)
    signed = np.where(lanes < half, lanes, lanes - length)

    def rows_of(groups):
        return [x for rows in groups for f in rows for x in (f, -f)]

    kept_rows = plain + rows_of(hosts)
    order = np.array(kept_rows + rows_of(guests))
    square = np.array(kept_rows)[:, None] ** 2 + signed[None, :] ** 2
    keep = np.ones((len(hosts), group, length), np.float32)
    moves = {}
    for q in range(pairs):
        free = {h: length - 1 - 2 * reach[rows[q]] for h, rows in enumerate(hosts)}
        for g, rows in enumerate(guests):
            f = rows[q]
            at, end = -reach[f], reach[f]
            while at <= end:
                need = end - at + 1
                if not free:
                    return None
                fits = [h for h in free if free[h] >= need]
                h = min(fits, key=lambda h: free[h]) if fits else max(free, key=lambda h: free[h])
                count = min(need, free.pop(h))
                start = reach[hosts[h][q]] + 1
                shift = (start - at) % length
                mask = moves.setdefault((h, g, shift), np.zeros((group, length), np.float32))
                cells = np.arange(start, start + count)
                for e in range(2):
                    mask[2 * q + e, cells] = 1.0
                    keep[h, 2 * q + e, cells] = 0.0
                    square[(first + h) * group + 2 * q + e, cells] = (
                        f * f + np.arange(at, at + count) ** 2)
                at += count
    plan = tuple(sorted(moves))
    masks = np.stack([moves[m] for m in plan] + list(keep))
    return order % length, first, plan, masks, square.astype(np.int32)


def split(field):
    high = field.astype(jnp.bfloat16)
    return high, (field - high.astype(jnp.float32)).astype(jnp.bfloat16)


def left_dot(table_ref, field):
    high, low = split(field)
    size = table_ref.shape[1] // 2
    th, tl = table_ref[:, :size], table_ref[:, size:]
    return jnp.dot(
        jnp.concatenate([th, th, tl], axis=1), jnp.concatenate([high, low, high], axis=0),
        preferred_element_type=jnp.float32)


def right_dot(field, table_ref):
    high, low = split(field)
    size = table_ref.shape[0] // 2
    th, tl = table_ref[:size], table_ref[size:]
    return jnp.dot(
        jnp.concatenate([high, low, high], axis=1), jnp.concatenate([th, th, tl], axis=0),
        preferred_element_type=jnp.float32)


def main_kernel(
    size_y, size_z, step, first, plan,
    u_hbm, pot_ref, cut_ref, sq_ref, xf_ref, xi_ref, lf_ref, li_ref, yf_ref, yi_ref, mask_ref,
    out_hbm, stat_ref,
    u, a1, r1, a2, r2, r3, o, sums, own, every,
    s1, q1, s2, q2, s3, q3, s4, q4, iu, io, sg, qg,
):
    me_y, me_z = lax.axis_index("py"), lax.axis_index("pz")
    _, _, slots, rows_z, rows_y, length = u.shape
    chunks = rows_z // step
    units = slots * chunks
    rows_k = sq_ref.shape[1]
    unit = 2 * step * rows_k
    pitch = a2.shape[1] // size_z
    blocks = size_z * chunks
    hosts = rows_k - first
    groups = length // size_z - rows_k
    count = size_y * size_z
    bands = size_y * slots

    def load(s, c):
        zs = pl.ds(c * step, step)
        return pltpu.make_async_copy(u_hbm.at[:, :, s, zs], u.at[:, :, s, zs], iu.at[s, c])

    def save(s, c):
        zs = pl.ds(c * step, step)
        return pltpu.make_async_copy(o.at[:, :, s, zs], out_hbm.at[:, :, s, zs], io.at[s, c])

    barrier = pltpu.get_barrier_semaphore()
    for d in range(1, size_z):
        pl.semaphore_signal(barrier, inc=1, device_id={"pz": (me_z + d) % size_z}, device_id_type=MESH)
    for d in range(1, size_y):
        pl.semaphore_signal(barrier, inc=1, device_id={"py": (me_y + d) % size_y}, device_id_type=MESH)
    for s in range(slots):
        for c in range(chunks):
            load(s, c).start()
    pl.semaphore_wait(barrier, size_y + size_z - 2)

    def copy1(s, c, d):
        to = (me_y + d) % size_y
        return pltpu.make_async_remote_copy(
            src_ref=a1.at[:, to, s, pl.ds(c * step, step)],
            dst_ref=r1.at[:, s, pl.ds(c * step, step), me_y],
            send_sem=s1.at[s, c, d - 1], recv_sem=q1.at[s, c, d - 1],
            device_id={"py": to}, device_id_type=MESH)

    def rows2(m, c):
        return pl.ds(pl.multiple_of(m * pitch + c * unit, 8), unit)

    def rows_r(m, c):
        return pl.ds(pl.multiple_of((m * chunks + c) * unit, 8), unit)

    def copy2(s, c, d):
        to = (me_z + d) % size_z
        return pltpu.make_async_remote_copy(
            src_ref=a2.at[s, rows2(to, c)], dst_ref=r2.at[s, rows_r(me_z, c)],
            send_sem=s2.at[s, c, d - 1], recv_sem=q2.at[s, c, d - 1],
            device_id={"pz": to}, device_id_type=MESH)

    def copy3(s, c, d):
        to = (me_z + d) % size_z
        return pltpu.make_async_remote_copy(
            src_ref=r2.at[s, rows_r(to, c)], dst_ref=r3.at[s, rows2(me_z, c)],
            send_sem=s3.at[s, c, d - 1], recv_sem=q3.at[s, c, d - 1],
            device_id={"pz": to}, device_id_type=MESH)

    def copy4(s, c, d):
        to = (me_y + d) % size_y
        return pltpu.make_async_remote_copy(
            src_ref=r1.at[:, s, pl.ds(c * step, step), to],
            dst_ref=o.at[:, me_y, s, pl.ds(c * step, step)],
            send_sem=s4.at[s, c, d - 1], recv_sem=q4.at[s, c, d - 1],
            device_id={"py": to}, device_id_type=MESH)

    order_z = sorted(range(1, size_z), key=lambda d: -min(d, size_z - d))
    order_y = sorted(range(1, size_y), key=lambda d: -min(d, size_y - d))

    def forward_x(i):
        s, c = i // chunks, i % chunks
        load(s, c).wait()
        zs = pl.ds(c * step, step)
        for d in order_y + [0]:
            to = (me_y + d) % size_y
            rows = jnp.concatenate(
                [u[p, to, s, zs].reshape(step * rows_y, length) for p in range(2)], axis=1)
            done = right_dot(rows, xf_ref)
            for p in range(2):
                part = done[:, p * length : (p + 1) * length].reshape(step, rows_y, length)
                if d == 0:
                    r1[p, s, zs, me_y] = part
                else:
                    a1[p, to, s, zs] = part
            if d > 0:
                copy1(s, c, d).start()

    def forward_y(i):
        s, c = i // chunks, i % chunks
        for d in range(1, size_y):
            copy1(s, c, d).wait_recv()
        for z in range(0, step, 2):
            sides = []
            for e in range(2):
                sides.append(jnp.concatenate(
                    [r1[p, s, c * step + z + e].reshape(length, length) for p in range(2)], axis=0))
            done = left_dot(yf_ref, jnp.concatenate(sides, axis=1))
            for p in range(2):
                for e in range(2):
                    part = done[p * length : (p + 1) * length, e * length : (e + 1) * length]
                    part = [part[g * size_z : (g + 1) * size_z] for g in range(rows_k + groups)]
                    for h in range(hosts):
                        part[first + h] = part[first + h] * mask_ref[len(plan) + h]
                    for t, (h, g, shift) in enumerate(plan):
                        part[first + h] = part[first + h] + pltpu.roll(
                            part[rows_k + g], shift, axis=1) * mask_ref[t]
                    for g in range(rows_k):
                        a2[s, pl.ds(c * unit + g * 2 * step + p * step + z + e, size_z, stride=pitch)] = part[g]
        for d in order_z:
            copy2(s, c, d).start()
        r2[s, rows_r(me_z, c)] = a2[s, rows2(me_z, c)]

    ahead = min(2, units)
    for i in range(ahead):
        forward_x(i)

    def forward_both(i, carry):
        forward_x(i + ahead)
        forward_y(i)
        return carry
    lax.fori_loop(0, units - ahead, forward_both, 0)

    def forward_rest(i, carry):
        forward_y(i)
        return carry
    lax.fori_loop(units - ahead, units, forward_rest, 0)

    kz = lax.broadcasted_iota(jnp.int32, (length, length), 0)
    kz_sq = signed_square(kz, length)

    def z_rows(s, ks):
        def at(k, p, i):
            return pl.ds(k * 2 * step + p * step + i, blocks, stride=unit)
        sides, weights = [], []
        for k in ks:
            sides.append(jnp.concatenate(
                [r2[s, at(k, p, i)] for p in range(2) for i in range(step)], axis=0))
            weights.append(weigh(kz_sq + sq_ref[me_z, pl.ds(k, 1)], cut_ref, length))
        weight = jnp.concatenate(weights, axis=1)
        spectrum = left_dot(lf_ref, jnp.concatenate(sides, axis=1))
        done = left_dot(li_ref, spectrum * jnp.concatenate([weight, weight], axis=0))
        for e, k in enumerate(ks):
            for p in range(2):
                for i in range(step):
                    r2[s, at(k, p, i)] = done[
                        p * length + i * blocks : p * length + (i + 1) * blocks,
                        e * length : (e + 1) * length]

    for s in range(slots):
        def arrive2(c, carry):
            for d in range(1, size_z):
                copy2(s, c, d).wait_recv()
            return carry
        lax.fori_loop(0, chunks, arrive2, 0)

        def both_z(h, carry):
            z_rows(s, (2 * h, 2 * h + 1))
            return carry
        lax.fori_loop(0, rows_k // 2, both_z, 0)
        if rows_k % 2:
            z_rows(s, (rows_k - 1,))

        def leave3(c, carry):
            for d in order_z:
                copy3(s, c, d).start()
            r3[s, rows2(me_z, c)] = r2[s, rows_r(me_z, c)]
            return carry
        lax.fori_loop(0, chunks, leave3, 0)

    def inverse_y(i):
        s, c = i // chunks, i % chunks
        for d in range(1, size_z):
            copy3(s, c, d).wait_recv()
        for z in range(0, step, 2):
            sides = []
            for e in range(2):
                both = []
                for p in range(2):
                    part = [r3[s, pl.ds(c * unit + g * 2 * step + p * step + z + e, size_z, stride=pitch)]
                            for g in range(rows_k)]
                    guests = [None] * groups
                    for t, (h, g, shift) in enumerate(plan):
                        moved = pltpu.roll(part[first + h] * mask_ref[t], length - shift, axis=1)
                        guests[g] = moved if guests[g] is None else guests[g] + moved
                    for h in range(hosts):
                        part[first + h] = part[first + h] * mask_ref[len(plan) + h]
                    both += part + guests
                sides.append(jnp.concatenate(both, axis=0))
            done = left_dot(yi_ref, jnp.concatenate(sides, axis=1))
            for p in range(2):
                for e in range(2):
                    part = done[p * length : (p + 1) * length, e * length : (e + 1) * length]
                    r1[p, s, c * step + z + e] = part.reshape(size_y, rows_y, length)
        for d in order_y:
            copy4(s, c, d).start()
        zs = pl.ds(c * step, step)
        o[:, me_y, s, zs] = r1[:, s, zs, me_y]

    def inverse_x(i):
        s, c = i // chunks, i % chunks
        zs = pl.ds(c * step, step)
        area = step * rows_y
        pot = pot_ref[zs].reshape(area, length)
        for d in range(size_y):
            owner = (me_y + size_y - d) % size_y
            if d > 0:
                copy4(s, c, d).wait_recv()
            rows = jnp.concatenate(
                [o[p, owner, s, zs].reshape(area, length) for p in range(2)], axis=1)
            done = right_dot(rows, xi_ref)
            fields, results = [], []
            for p in range(2):
                field = u[p, owner, s, zs].reshape(area, length)
                part = done[:, p * length : (p + 1) * length] + pot * field
                o[p, owner, s, zs] = part.reshape(step, rows_y, length)
                fields.append(field.reshape(area // 8, 8, length))
                results.append(part.reshape(area // 8, 8, length))

            def total(values):
                return jnp.sum(values[0] + values[1], axis=0)
            norm = total([f * f for f in fields])
            corr = total([f * r for f, r in zip(fields, results)])
            shift = jnp.where(norm > 0.0, corr / jnp.where(norm > 0.0, norm, 1.0), 0.0)
            gaps = [r - shift[None] * f for f, r in zip(fields, results)]
            values = (norm, corr, shift, total([g * g for g in gaps]),
                      total([g * f for g, f in zip(gaps, fields)]))
            for n, value in enumerate(values):
                sums[n, owner, s, c] = value
        save(s, c).start()

    inverse_y(0)

    def inverse_both(i, carry):
        inverse_y(i)
        inverse_x(i - 1)
        return carry
    lax.fori_loop(1, units, inverse_both, 0)
    inverse_x(units - 1)

    norm, corr, shift, rest_sq, rest_dot = (
        sums[n].reshape(bands, chunks * 8, length) for n in range(5))

    def of_band(value):
        return jnp.sum(jnp.sum(value, axis=1), axis=1, keepdims=True)
    norm_own, corr_own = of_band(norm), of_band(corr)
    shift_own = jnp.where(norm_own > 0.0, corr_own / jnp.where(norm_own > 0.0, norm_own, 1.0), 0.0)
    gap = shift - shift_own[:, :, None]
    sq_own = of_band(rest_sq + gap * (2.0 * rest_dot + gap * norm))
    dot_own = of_band(rest_dot + gap * norm)
    line = lax.broadcasted_iota(jnp.int32, (bands, length), 0)
    lane = lax.broadcasted_iota(jnp.int32, (bands, length), 1)
    packed = jnp.zeros((bands, length), jnp.float32)
    for n, value in enumerate((norm_own, corr_own, shift_own, sq_own, dot_own)):
        packed = jnp.where(lane == n * bands + line, value, packed)
    own[...] = jnp.sum(packed, axis=0, keepdims=True)
    me = me_y * size_z + me_z

    def tell(t):
        to = (me + t) % count
        return pltpu.make_async_remote_copy(
            src_ref=own, dst_ref=every.at[me], send_sem=sg.at[t], recv_sem=qg.at[t],
            device_id={"py": to // size_z, "pz": to % size_z}, device_id_type=MESH)

    def tell_start(t, carry):
        tell(t).start()
        return carry
    lax.fori_loop(1, count, tell_start, 0)
    every[me] = own[...]

    def settle(i, carry):
        s, c = i // chunks, i % chunks
        for d in range(1, size_y):
            copy1(s, c, d).wait_send()
            copy4(s, c, d).wait_send()
        for d in range(1, size_z):
            copy2(s, c, d).wait_send()
            copy3(s, c, d).wait_send()
        save(s, c).wait()
        return carry
    lax.fori_loop(0, units, settle, 0)

    def tell_end(t, carry):
        tell(t).wait()
        return carry
    lax.fori_loop(1, count, tell_end, 0)

    table = every[...].reshape(count, length)
    total = jnp.sum(table, axis=0, keepdims=True)

    def kind(value, n):
        return pltpu.roll(value, length - n * bands, axis=1)
    used = lax.broadcasted_iota(jnp.int32, (1, length), 1) < bands
    norm_sq = jnp.where(used, total, 1.0)
    corr_all = kind(jnp.broadcast_to(total, (8, length)), 1)[:1]
    rayleigh = jnp.where(used, corr_all, 0.0) / norm_sq
    gap = kind(table, 2) - rayleigh
    residual = kind(table, 3) + gap * (2.0 * kind(table, 4) + gap * table)
    residual = jnp.maximum(jnp.sum(residual, axis=0, keepdims=True), 0.0)
    residual = jnp.sqrt(jnp.where(used, residual, 0.0) / norm_sq)
    stat_ref[...] = jnp.concatenate(
        [jnp.broadcast_to(rayleigh, (4, length)), jnp.broadcast_to(residual, (4, length))], axis=0)


def two_parts(table):
    table = np.asarray(table, np.float64).astype(np.float32)
    high = table.astype(jnp.bfloat16)
    low = (table - high.astype(np.float32)).astype(jnp.bfloat16)
    return high, low


def exact_matrix(length, inverse):
    counter = np.arange(length)
    angle = 2.0 * math.pi / length * (counter[:, None] * counter[None, :] % length)
    if inverse:
        cosines, sines = np.cos(angle) / length, np.sin(angle) / length
    else:
        cosines, sines = np.cos(angle), -np.sin(angle)
    return np.block([[cosines, sines], [-sines, cosines]])


def fused_hamiltonian(wavefunctions, potential, cutoff_sq, folding, step):
    order, first, plan, masks, square = folding
    _, bands, rows_z, rows_y, length = wavefunctions.shape
    size_y, size_z = lax.axis_size("py"), lax.axis_size("pz")
    slots = bands // size_y
    rows_k = square.shape[0] // size_z
    chunks = rows_z // step
    unit = 2 * step * rows_k
    pitch = chunks * unit + 8
    blocks = size_z * chunks
    count = size_y * size_z
    xf, xi = exact_matrix(length, False), exact_matrix(length, True)
    both_y = np.concatenate([order, order + length])
    order_z = (step * np.arange(blocks)[None, :] + np.arange(step)[:, None]).reshape(-1)
    both_z = np.concatenate([order_z, order_z + length])
    tables = [np.concatenate(two_parts(t), axis=0) for t in (xf, xi)]
    tables += [np.concatenate(two_parts(t), axis=1)
               for t in (xf.T[:, both_z], xi.T[both_z], xf.T[both_y], xi.T[:, both_y])]
    tables = [jnp.asarray(t) for t in tables]
    squares = np.ascontiguousarray(square.reshape(rows_k, size_z, length).swapaxes(0, 1))
    field = wavefunctions.reshape(2, size_y, slots, rows_z, rows_y, length)
    vmem = pl.BlockSpec(memory_space=pltpu.VMEM)
    smem = pl.BlockSpec(memory_space=pltpu.SMEM)
    hbm = pl.BlockSpec(memory_space=pl.ANY)
    near = pltpu.SemaphoreType.DMA((slots, chunks, size_y - 1))
    far = pltpu.SemaphoreType.DMA((slots, chunks, size_z - 1))
    here = pltpu.SemaphoreType.DMA((slots, chunks))
    each = pltpu.SemaphoreType.DMA((count,))
    f32 = jnp.float32
    applied, stats = pl.pallas_call(
        functools.partial(main_kernel, size_y, size_z, step, first, plan),
        out_shape=(jax.ShapeDtypeStruct(field.shape, f32), jax.ShapeDtypeStruct((8, length), f32)),
        in_specs=[hbm, vmem, smem] + [vmem] * 8,
        out_specs=(hbm, vmem),
        scratch_shapes=[
            pltpu.VMEM(field.shape, f32),
            pltpu.VMEM(field.shape, f32),
            pltpu.VMEM((2, slots, rows_z, size_y, rows_y, length), f32),
            pltpu.VMEM((slots, size_z * pitch, length), f32),
            pltpu.VMEM((slots, blocks * unit, length), f32),
            pltpu.VMEM((slots, size_z * pitch, length), f32),
            pltpu.VMEM(field.shape, f32),
            pltpu.VMEM((5, size_y, slots, chunks, 8, length), f32),
            pltpu.VMEM((1, length), f32),
            pltpu.VMEM((count, 1, length), f32),
            near, near, far, far, far, far, near, near, here, here, each, each,
        ],
        compiler_params=pltpu.CompilerParams(
            collective_id=0, has_side_effects=True, vmem_limit_bytes=67043328),
    )(field, potential, cutoff_sq, jnp.asarray(squares), *tables, jnp.asarray(masks))
    return applied.reshape(wavefunctions.shape), stats[0, :bands], stats[4, :bands]


def gather_kernel(size_y, size_z, own_ref, out_ref, send, recv):
    me_y, me_z = lax.axis_index("py"), lax.axis_index("pz")
    me = me_y * size_z + me_z
    count = size_y * size_z
    barrier = pltpu.get_barrier_semaphore()

    def target(t):
        to = (me + t) % count
        return {"py": to // size_z, "pz": to % size_z}

    def greet(t, carry):
        pl.semaphore_signal(barrier, inc=1, device_id=target(t), device_id_type=MESH)
        return carry
    lax.fori_loop(1, count, greet, 0)
    pl.semaphore_wait(barrier, count - 1)

    def copy(t):
        return pltpu.make_async_remote_copy(
            src_ref=own_ref, dst_ref=out_ref.at[me], send_sem=send.at[t], recv_sem=recv.at[t],
            device_id=target(t), device_id_type=MESH)

    def leave(t, carry):
        copy(t).start()
        return carry
    lax.fori_loop(1, count, leave, 0)
    out_ref[me] = own_ref[...]

    def arrive(t, carry):
        copy(t).wait()
        return carry
    lax.fori_loop(1, count, arrive, 0)


def gather_sums(sums):
    size_y, size_z = lax.axis_size("py"), lax.axis_size("pz")
    count = size_y * size_z
    kinds, bands = sums.shape
    if count > 64:
        return lax.all_gather(sums, ("py", "pz"))
    own = jnp.pad(sums, ((0, 8 - kinds), (0, 128 - bands)))
    vmem = pl.BlockSpec(memory_space=pltpu.VMEM)
    every = pl.pallas_call(
        functools.partial(gather_kernel, size_y, size_z),
        out_shape=jax.ShapeDtypeStruct((count, 8, 128), jnp.float32),
        in_specs=[vmem],
        out_specs=vmem,
        scratch_shapes=[pltpu.SemaphoreType.DMA((count,)), pltpu.SemaphoreType.DMA((count,))],
        compiler_params=pltpu.CompilerParams(collective_id=1, has_side_effects=True),
    )(own)
    return every[:, :kinds, :bands]


def weigh(total, cutoff_sq, length):
    keep = (total <= cutoff_sq[0]).astype(jnp.float32)
    return 0.5 * (math.pi / length) ** 2 * total.astype(jnp.float32) * keep


def plain_kinetic(wavefunctions, kinetic, forward, inverse):
    along_x = "bzyn,kn->bzyk"
    along_y = "bznx,kn->bzkx"
    along_z = "bnyx,kn->bkyx"
    pair = (wavefunctions[0], wavefunctions[1])
    pair = transform(along_x, pair, forward)
    pair = exchange(pair, "py", 0, 2)
    pair = transform(along_y, pair, forward)
    pair = exchange(pair, "pz", 2, 1)
    pair = transform(along_z, pair, forward)
    pair = tuple(part * jnp.swapaxes(kinetic, 0, 1)[None] for part in pair)
    pair = transform(along_z, pair, inverse)
    pair = exchange(pair, "pz", 1, 2)
    pair = transform(along_y, pair, inverse)
    pair = exchange(pair, "py", 2, 0)
    pair = transform(along_x, pair, inverse)
    return jnp.stack(pair)


def body(wavefunctions, potential, cutoff_sq, locked_mask):
    _, bands, rows_z, rows_y, length = wavefunctions.shape
    size_y, size_z = lax.axis_size("py"), lax.axis_size("pz")
    step = 4
    unlocked = 1.0 - locked_mask.astype(jnp.float32)
    fits = size_z == 8 and bands == 8 and length % 128 == 0 and bands % size_y == 0
    fits = fits and rows_z % step == 0 and step * rows_y % 8 == 0
    folding = None
    if fits:
        folding = fold_rows(length, size_z, 3 * size_z) or fold_rows(length, size_z, 2 * size_z)
    if folding is not None:
        applied, rayleigh, residual = fused_hamiltonian(
            wavefunctions, potential, cutoff_sq, folding, step)
        return (applied, rayleigh, residual * unlocked)
    forward = make_tables(length, False)
    inverse = make_tables(length, True)
    rows = length // size_z
    full_sq = signed_square(jnp.arange(length, dtype=jnp.int32), length)
    own = lax.axis_index("pz") * rows + jnp.arange(rows, dtype=jnp.int32)
    own_sq = signed_square(own, length)
    total = own_sq[:, None, None] + full_sq[None, :, None] + full_sq[None, None, :]
    kinetic = weigh(total, cutoff_sq, length)
    back = plain_kinetic(wavefunctions, kinetic, forward, inverse)
    applied = back + potential[None, None] * wavefunctions
    norm_own = jnp.sum(wavefunctions * wavefunctions, axis=(0, 2, 3, 4))
    corr_own = jnp.sum(wavefunctions * applied, axis=(0, 2, 3, 4))
    shift = jnp.where(norm_own > 0.0, corr_own / jnp.where(norm_own > 0.0, norm_own, 1.0), 0.0)
    rest = applied - shift[None, :, None, None, None] * wavefunctions
    rest_sq = jnp.sum(rest * rest, axis=(0, 2, 3, 4))
    rest_dot = jnp.sum(rest * wavefunctions, axis=(0, 2, 3, 4))
    sums = jnp.stack([norm_own, corr_own, shift, rest_sq, rest_dot])
    every = gather_sums(sums)
    norm_all, corr_all, shift_all, sq_all, dot_all = (every[:, i] for i in range(5))
    norm_sq = jnp.sum(norm_all, axis=0)
    rayleigh = jnp.sum(corr_all, axis=0) / norm_sq
    gap = shift_all - rayleigh[None]
    residual_sq = jnp.sum(sq_all + 2.0 * gap * dot_all + gap * gap * norm_all, axis=0)
    residual_sq = jnp.maximum(residual_sq, 0.0)
    residual_norm = jnp.sqrt(residual_sq / norm_sq) * unlocked
    return (applied, rayleigh, residual_norm)


def solution(mesh):
    in_specs = (P(None, None, "pz", "py", None), P("pz", "py", None), P(), P())
    out_specs = (P(None, None, "pz", "py", None), P(), P())
    return jax.shard_map(body, mesh=mesh, in_specs=in_specs, out_specs=out_specs, check_vma=False)
```

time: 227 us -> 194 us (0.85)
  Pallas kernels: 207 us -> 185 us
  other arithmetic: 11.8 us -> 1.21 us
    pallas_call x2 -> x1, Pallas kernels: 207 us -> 185 us  [fused_hamiltonian(): pl.pallas_call(functools.partial(main_kernel, size_y, size_z, step, first...]
    reduce_sum x4 -> x0, other arithmetic: 6.95 us -> none  [the longest x1 5.29 us: body(): corr_own = jnp.sum(wavefunctions * applied, axis=(0, 2, 3, 4))]
    unnamed x12 -> x1, local copies, waits for them, and re-layouts: 0.39 us -> 4.8 us
    gather x3 -> x0, local copies, waits for them, and re-layouts: 3.49 us -> none  [the longest x2 1.82 us: fused_kinetic(): xi.T[:, both]]
where the time goes in v1:
time: 194 us
  Pallas kernels  185 us (95%)
  local copies, waits for them, and re-layouts  5.99 us (3%)
    pallas_call x1, Pallas kernels, fused_hamiltonian(): pl.pallas_call(functools.partial(main_kernel, size_y, size_z, step, first...  185 us
    unnamed x1, local copies, waits for them, and re-layouts  4.8 us

profile of v1, /device:TPU:0, one launch (start us, length us, event | category | flops | bytes accessed | tf_op | source)
XLA Modules:
  0.0 193.6 jit_solution(4439923572964804304)
XLA Ops:
  1.3 185.1 %shard_map.139 = (f32[2,4,2,16,32,128]{5,4,3,2,1,0:T(8,128)}, f32[8,128]{1,0:T(8,128)}) custom-call(f32[2,4,2,16,32,128]{5,4,3,2,1,0:T(8,128)} %bitcast.6, f32[16,32,128]{2,1,0:T(8,128)} %pot_ref.1, s32[1]{0:T(128)S(6)} %copy.16.cut_ref, s32[8,13,128]{2,1,0:T(8,128)} %constant.24.clone.sq_ref, bf16[512,256]{1,0:T(8,128)(2,1)} %constant.18.clone.xf_ref, ...), custom_call_target="tpu_custom_call" | custom-call | tf_op jit(solution)/shard_map/pallas_call | solution.py:489
  186.4 1.2 bitcast_multiply_fusion
  187.6 1.2 slice_bitcast_fusion
  188.8 4.8 %copy.17 = f32[2,8,16,32,128]{4,3,2,1,0:T(8,128)} copy(f32[2,8,16,32,128]{4,3,2,1,0:T(8,128)} %bitcast.7) | data formatting | bytes 8388608

commit v2 on v1

--- a/solution.py
+++ b/solution.py
@@ -48,6 +48,9 @@
     cosines, sines = tables
     top = jnp.concatenate([cosines, sines], axis=1)
     return jnp.concatenate([top, jnp.concatenate([-sines, cosines], axis=1)], axis=0)
+
+
+WINDOW = 2
 
 
 def fold_rows(length, lanes_of, extra):
@@ -129,12 +132,17 @@
         preferred_element_type=jnp.float32)
 
 
+def await_all(ref, sem):
+    pltpu.make_async_copy(ref, ref, sem).wait()
+
+
 def main_kernel(
-    size_y, size_z, step, first, plan,
-    u_hbm, pot_ref, cut_ref, sq_ref, xf_ref, xi_ref, lf_ref, li_ref, yf_ref, yi_ref, mask_ref,
-    out_hbm, stat_ref,
-    u, a1, r1, a2, r2, r3, o, sums, own, every,
-    s1, q1, s2, q2, s3, q3, s4, q4, iu, io, sg, qg,
+    size_y, size_z, step, first, plan, window,
+    u_hbm, cut_ref, locked_ref, xf_hbm, yf_hbm, mask_hbm, lf_hbm, li_hbm, sq_hbm, yi_hbm, xi_hbm, pot_hbm,
+    o, every,
+    u, xf_ref, yf_ref, mask_ref, lf_ref, li_ref, sq_ref, yi_ref, xi_ref, pot_ref,
+    a1, r1, a2, r2, r3, sums, own,
+    s1, q1, s2, q2, s3, q3, s4, q4, iu, it, sg, qg,
 ):
     me_y, me_z = lax.axis_index("py"), lax.axis_index("pz")
     _, _, slots, rows_z, rows_y, length = u.shape
@@ -153,26 +161,27 @@
         zs = pl.ds(c * step, step)
         return pltpu.make_async_copy(u_hbm.at[:, :, s, zs], u.at[:, :, s, zs], iu.at[s, c])
 
-    def save(s, c):
-        zs = pl.ds(c * step, step)
-        return pltpu.make_async_copy(o.at[:, :, s, zs], out_hbm.at[:, :, s, zs], io.at[s, c])
-
     barrier = pltpu.get_barrier_semaphore()
     for d in range(1, size_z):
         pl.semaphore_signal(barrier, inc=1, device_id={"pz": (me_z + d) % size_z}, device_id_type=MESH)
     for d in range(1, size_y):
         pl.semaphore_signal(barrier, inc=1, device_id={"py": (me_y + d) % size_y}, device_id_type=MESH)
-    for s in range(slots):
-        for c in range(chunks):
-            load(s, c).start()
-    pl.semaphore_wait(barrier, size_y + size_z - 2)
+    pairs = ((xf_hbm, xf_ref), (yf_hbm, yf_ref), (mask_hbm, mask_ref), (lf_hbm, lf_ref), (li_hbm, li_ref),
+             (sq_hbm, sq_ref), (yi_hbm, yi_ref), (xi_hbm, xi_ref), (pot_hbm, pot_ref))
+    fetches = [pltpu.make_async_copy(src, dst, it.at[n]) for n, (src, dst) in enumerate(pairs)]
+    fetches[0].start()
+    load(0, 0).start()
+    for fetch in fetches[1:]:
+        fetch.start()
+    for i in range(1, units):
+        load(i // chunks, i % chunks).start()
 
     def copy1(s, c, d):
         to = (me_y + d) % size_y
         return pltpu.make_async_remote_copy(
             src_ref=a1.at[:, to, s, pl.ds(c * step, step)],
             dst_ref=r1.at[:, s, pl.ds(c * step, step), me_y],
-            send_sem=s1.at[s, c, d - 1], recv_sem=q1.at[s, c, d - 1],
+            send_sem=s1, recv_sem=q1.at[s, c],
             device_id={"py": to}, device_id_type=MESH)
 
     def rows2(m, c):
@@ -185,14 +194,14 @@
         to = (me_z + d) % size_z
         return pltpu.make_async_remote_copy(
             src_ref=a2.at[s, rows2(to, c)], dst_ref=r2.at[s, rows_r(me_z, c)],
-            send_sem=s2.at[s, c, d - 1], recv_sem=q2.at[s, c, d - 1],
+            send_sem=s2, recv_sem=q2.at[s, c],
             device_id={"pz": to}, device_id_type=MESH)
 
     def copy3(s, c, d):
         to = (me_z + d) % size_z
         return pltpu.make_async_remote_copy(
             src_ref=r2.at[s, rows_r(to, c)], dst_ref=r3.at[s, rows2(me_z, c)],
-            send_sem=s3.at[s, c, d - 1], recv_sem=q3.at[s, c, d - 1],
+            send_sem=s3, recv_sem=q3.at[s, c],
             device_id={"pz": to}, device_id_type=MESH)
 
     def copy4(s, c, d):
@@ -200,13 +209,13 @@
         return pltpu.make_async_remote_copy(
             src_ref=r1.at[:, s, pl.ds(c * step, step), to],
             dst_ref=o.at[:, me_y, s, pl.ds(c * step, step)],
-            send_sem=s4.at[s, c, d - 1], recv_sem=q4.at[s, c, d - 1],
+            send_sem=s4, recv_sem=q4.at[s, c],
             device_id={"py": to}, device_id_type=MESH)
 
     order_z = sorted(range(1, size_z), key=lambda d: -min(d, size_z - d))
     order_y = sorted(range(1, size_y), key=lambda d: -min(d, size_y - d))
 
-    def forward_x(i):
+    def forward_x(i, leave):
         s, c = i // chunks, i % chunks
         load(s, c).wait()
         zs = pl.ds(c * step, step)
@@ -221,13 +230,12 @@
                     r1[p, s, zs, me_y] = part
                 else:
                     a1[p, to, s, zs] = part
-            if d > 0:
+            if d > 0 and leave:
                 copy1(s, c, d).start()
 
     def forward_y(i):
         s, c = i // chunks, i % chunks
-        for d in range(1, size_y):
-            copy1(s, c, d).wait_recv()
+        await_all(a1.at[:, pl.ds(0, size_y - 1), s, pl.ds(c * step, step)], q1.at[s, c])
         for z in range(0, step, 2):
             sides = []
             for e in range(2):
@@ -245,24 +253,21 @@
                             part[rows_k + g], shift, axis=1) * mask_ref[t]
                     for g in range(rows_k):
                         a2[s, pl.ds(c * unit + g * 2 * step + p * step + z + e, size_z, stride=pitch)] = part[g]
+        r2[s, rows_r(me_z, c)] = a2[s, rows2(me_z, c)]
+
+    def leave2(i):
         for d in order_z:
-            copy2(s, c, d).start()
-        r2[s, rows_r(me_z, c)] = a2[s, rows2(me_z, c)]
-
-    ahead = min(2, units)
-    for i in range(ahead):
-        forward_x(i)
-
-    def forward_both(i, carry):
-        forward_x(i + ahead)
-        forward_y(i)
-        return carry
-    lax.fori_loop(0, units - ahead, forward_both, 0)
-
-    def forward_rest(i, carry):
-        forward_y(i)
-        return carry
-    lax.fori_loop(units - ahead, units, forward_rest, 0)
+            copy2(i // chunks, i % chunks, d).start()
+
+    def arrive2(i):
+        await_all(a2.at[0, pl.ds(0, (size_z - 1) * unit)], q2.at[i // chunks, i % chunks])
+
+    def leave3(i):
+        for d in order_z:
+            copy3(i // chunks, i % chunks, d).start()
+
+    def arrive3(i):
+        await_all(a2.at[0, pl.ds(0, (size_z - 1) * unit)], q3.at[i // chunks, i % chunks])
 
     kz = lax.broadcasted_iota(jnp.int32, (length, length), 0)
     kz_sq = signed_square(kz, length)
@@ -285,31 +290,21 @@
                         p * length + i * blocks : p * length + (i + 1) * blocks,
                         e * length : (e + 1) * length]
 
-    for s in range(slots):
-        def arrive2(c, carry):
-            for d in range(1, size_z):
-                copy2(s, c, d).wait_recv()
-            return carry
-        lax.fori_loop(0, chunks, arrive2, 0)
-
-        def both_z(h, carry):
+    def both_z(s):
+        def two_rows(h, carry):
             z_rows(s, (2 * h, 2 * h + 1))
             return carry
-        lax.fori_loop(0, rows_k // 2, both_z, 0)
+        lax.fori_loop(0, rows_k // 2, two_rows, 0)
         if rows_k % 2:
             z_rows(s, (rows_k - 1,))
 
-        def leave3(c, carry):
-            for d in order_z:
-                copy3(s, c, d).start()
+        def keep(c, carry):
             r3[s, rows2(me_z, c)] = r2[s, rows_r(me_z, c)]
             return carry
-        lax.fori_loop(0, chunks, leave3, 0)
+        lax.fori_loop(0, chunks, keep, 0)
 
     def inverse_y(i):
         s, c = i // chunks, i % chunks
-        for d in range(1, size_z):
-            copy3(s, c, d).wait_recv()
         for z in range(0, step, 2):
             sides = []
             for e in range(2):
@@ -340,10 +335,9 @@
         zs = pl.ds(c * step, step)
         area = step * rows_y
         pot = pot_ref[zs].reshape(area, length)
+        await_all(a1.at[:, pl.ds(0, size_y - 1), s, zs], q4.at[s, c])
         for d in range(size_y):
             owner = (me_y + size_y - d) % size_y
-            if d > 0:
-                copy4(s, c, d).wait_recv()
             rows = jnp.concatenate(
                 [o[p, owner, s, zs].reshape(area, length) for p in range(2)], axis=1)
             done = right_dot(rows, xi_ref)
@@ -365,15 +359,67 @@
                       total([g * f for g, f in zip(gaps, fields)]))
             for n, value in enumerate(values):
                 sums[n, owner, s, c] = value
-        save(s, c).start()
-
-    inverse_y(0)
-
-    def inverse_both(i, carry):
-        inverse_y(i)
-        inverse_x(i - 1)
-        return carry
-    lax.fori_loop(1, units, inverse_both, 0)
+
+    ahead = min(2, units)
+    fetches[0].wait()
+
+    def before(i, carry):
+        forward_x(i, False)
+        return carry
+    lax.fori_loop(0, ahead, before, 0)
+    pl.semaphore_wait(barrier, size_y + size_z - 2)
+
+    def depart(i, carry):
+        for d in order_y:
+            copy1(i // chunks, i % chunks, d).start()
+        return carry
+    lax.fori_loop(0, ahead, depart, 0)
+    for fetch in fetches[1:]:
+        fetch.wait()
+
+    def outward(i, carry):
+        @pl.when(i + ahead < units)
+        def _():
+            forward_x(i + ahead, True)
+        forward_y(i)
+
+        @pl.when(i >= window)
+        def _():
+            arrive2(i - window)
+        leave2(i)
+
+        @pl.when((i >= window) & ((i - window) % chunks == chunks - 1))
+        def _():
+            both_z((i - window) // chunks)
+        return carry
+    lax.fori_loop(0, units, outward, 0)
+
+    def homeward(i, carry):
+        @pl.when(i < window)
+        def _():
+            arrive2(units - window + i)
+
+        @pl.when(i >= window)
+        def _():
+            arrive3(i - window)
+
+        @pl.when(i < units)
+        def _():
+            leave3(i)
+
+        @pl.when(i == window - 1)
+        def _():
+            both_z(slots - 1)
+
+        @pl.when(i >= window)
+        def _():
+            inverse_y(i - window)
+
+        @pl.when(i > window)
+        def _():
+            inverse_x(i - window - 1)
+        return carry
+    lax.fori_loop(0, units + window, homeward, 0)
     inverse_x(units - 1)
 
     norm, corr, shift, rest_sq, rest_dot = (
@@ -397,7 +443,7 @@
     def tell(t):
         to = (me + t) % count
         return pltpu.make_async_remote_copy(
-            src_ref=own, dst_ref=every.at[me], send_sem=sg.at[t], recv_sem=qg.at[t],
+            src_ref=own, dst_ref=every.at[me], send_sem=sg, recv_sem=qg,
             device_id={"py": to // size_z, "pz": to % size_z}, device_id_type=MESH)
 
     def tell_start(t, carry):
@@ -405,39 +451,43 @@
         return carry
     lax.fori_loop(1, count, tell_start, 0)
     every[me] = own[...]
-
-    def settle(i, carry):
-        s, c = i // chunks, i % chunks
-        for d in range(1, size_y):
-            copy1(s, c, d).wait_send()
-            copy4(s, c, d).wait_send()
-        for d in range(1, size_z):
-            copy2(s, c, d).wait_send()
-            copy3(s, c, d).wait_send()
-        save(s, c).wait()
-        return carry
-    lax.fori_loop(0, units, settle, 0)
-
-    def tell_end(t, carry):
-        tell(t).wait()
-        return carry
-    lax.fori_loop(1, count, tell_end, 0)
-
-    table = every[...].reshape(count, length)
-    total = jnp.sum(table, axis=0, keepdims=True)
+    free = jnp.zeros((1, length), jnp.float32)
+
+    for n in range(bands):
+        free = jnp.where(lane[:1] == n, 1.0 - locked_ref[n].astype(jnp.float32), free)
+    every[count] = free
+    for sem in (s1, s4):
+        await_all(a1.at[:, pl.ds(0, size_y - 1)], sem)
+    for sem in (s2, s3):
+        await_all(a2.at[:, pl.ds(0, (size_z - 1) * chunks * unit)], sem)
+    for sem in (sg, qg):
+        await_all(every.at[pl.ds(0, count - 1)], sem)
+
+
+def finish_kernel(bands, applied_ref, every_ref, out_hbm, rayleigh_hbm, residual_hbm, ray, res, sems):
+    copies = [pltpu.make_async_copy(src, dst, sems.at[n]) for n, (src, dst) in enumerate(
+        ((applied_ref, out_hbm), (ray, rayleigh_hbm), (res, residual_hbm)))]
+    copies[0].start()
+    count, _, length = every_ref.shape
+    count = count - 1
+    table = every_ref[pl.ds(0, count)].reshape(count, length)
+    total = jnp.broadcast_to(jnp.sum(table, axis=0, keepdims=True), (8, length))
+    used = lax.broadcasted_iota(jnp.int32, (8, length), 1) < bands
 
     def kind(value, n):
         return pltpu.roll(value, length - n * bands, axis=1)
-    used = lax.broadcasted_iota(jnp.int32, (1, length), 1) < bands
     norm_sq = jnp.where(used, total, 1.0)
-    corr_all = kind(jnp.broadcast_to(total, (8, length)), 1)[:1]
-    rayleigh = jnp.where(used, corr_all, 0.0) / norm_sq
-    gap = kind(table, 2) - rayleigh
+    rayleigh = jnp.where(used, kind(total, 1), 0.0) / norm_sq
+    gap = kind(table, 2) - rayleigh[:1]
     residual = kind(table, 3) + gap * (2.0 * kind(table, 4) + gap * table)
     residual = jnp.maximum(jnp.sum(residual, axis=0, keepdims=True), 0.0)
     residual = jnp.sqrt(jnp.where(used, residual, 0.0) / norm_sq)
-    stat_ref[...] = jnp.concatenate(
-        [jnp.broadcast_to(rayleigh, (4, length)), jnp.broadcast_to(residual, (4, length))], axis=0)
+    ray[...] = rayleigh[:1, :bands]
+    res[...] = (residual[:1] * every_ref[count])[:, :bands]
+    for copy in copies[1:]:
+        copy.start()
+    for copy in copies:
+        copy.wait()
 
 
 def two_parts(table):
@@ -457,7 +507,7 @@
     return np.block([[cosines, sines], [-sines, cosines]])
 
 
-def fused_hamiltonian(wavefunctions, potential, cutoff_sq, folding, step):
+def fused_hamiltonian(wavefunctions, potential, cutoff_sq, locked_mask, folding, step):
     order, first, plan, masks, square = folding
     _, bands, rows_z, rows_y, length = wavefunctions.shape
     size_y, size_z = lax.axis_size("py"), lax.axis_size("pz")
@@ -477,37 +527,49 @@
                for t in (xf.T[:, both_z], xi.T[both_z], xf.T[both_y], xi.T[:, both_y])]
     tables = [jnp.asarray(t) for t in tables]
     squares = np.ascontiguousarray(square.reshape(rows_k, size_z, length).swapaxes(0, 1))
+    xf_t, xi_t, lf_t, li_t, yf_t, yi_t = tables
     field = wavefunctions.reshape(2, size_y, slots, rows_z, rows_y, length)
     vmem = pl.BlockSpec(memory_space=pltpu.VMEM)
     smem = pl.BlockSpec(memory_space=pltpu.SMEM)
-    hbm = pl.BlockSpec(memory_space=pl.ANY)
-    near = pltpu.SemaphoreType.DMA((slots, chunks, size_y - 1))
-    far = pltpu.SemaphoreType.DMA((slots, chunks, size_z - 1))
+    anywhere = pl.BlockSpec(memory_space=pl.ANY)
+    hbm = pl.BlockSpec(memory_space=pltpu.HBM)
     here = pltpu.SemaphoreType.DMA((slots, chunks))
-    each = pltpu.SemaphoreType.DMA((count,))
+    once = pltpu.SemaphoreType.DMA
     f32 = jnp.float32
-    applied, stats = pl.pallas_call(
-        functools.partial(main_kernel, size_y, size_z, step, first, plan),
-        out_shape=(jax.ShapeDtypeStruct(field.shape, f32), jax.ShapeDtypeStruct((8, length), f32)),
-        in_specs=[hbm, vmem, smem] + [vmem] * 8,
-        out_specs=(hbm, vmem),
-        scratch_shapes=[
-            pltpu.VMEM(field.shape, f32),
+    in_hbm = functools.partial(pltpu.with_memory_space_constraint, memory_space=pltpu.HBM)
+    in_vmem = functools.partial(pltpu.with_memory_space_constraint, memory_space=pltpu.VMEM)
+    operands = (xf_t, yf_t, jnp.asarray(masks), lf_t, li_t, jnp.asarray(squares), yi_t, xi_t, potential)
+    applied, every = pl.pallas_call(
+        functools.partial(main_kernel, size_y, size_z, step, first, plan, WINDOW),
+        out_shape=(pltpu.VMEM(field.shape, f32), pltpu.VMEM((count + 1, 1, length), f32)),
+        in_specs=[hbm, smem, smem] + [hbm] * len(operands),
+        out_specs=(vmem, vmem),
+        scratch_shapes=[pltpu.VMEM(field.shape, f32)]
+        + [pltpu.VMEM(x.shape, x.dtype) for x in operands]
+        + [
             pltpu.VMEM(field.shape, f32),
             pltpu.VMEM((2, slots, rows_z, size_y, rows_y, length), f32),
             pltpu.VMEM((slots, size_z * pitch, length), f32),
             pltpu.VMEM((slots, blocks * unit, length), f32),
             pltpu.VMEM((slots, size_z * pitch, length), f32),
-            pltpu.VMEM(field.shape, f32),
             pltpu.VMEM((5, size_y, slots, chunks, 8, length), f32),
             pltpu.VMEM((1, length), f32),
-            pltpu.VMEM((count, 1, length), f32),
-            near, near, far, far, far, far, near, near, here, here, each, each,
+            once, here, once, here, once, here, once, here, here,
+            pltpu.SemaphoreType.DMA((len(operands),)), once, once,
         ],
         compiler_params=pltpu.CompilerParams(
-            collective_id=0, has_side_effects=True, vmem_limit_bytes=67043328),
-    )(field, potential, cutoff_sq, jnp.asarray(squares), *tables, jnp.asarray(masks))
-    return applied.reshape(wavefunctions.shape), stats[0, :bands], stats[4, :bands]
+            collective_id=0, has_side_effects=True, vmem_limit_bytes=48 * 1024 * 1024),
+    )(in_hbm(field), cutoff_sq, locked_mask, *[in_hbm(x) for x in operands])
+    out, rayleigh, residual = pl.pallas_call(
+        functools.partial(finish_kernel, bands),
+        out_shape=(jax.ShapeDtypeStruct(field.shape, f32), jax.ShapeDtypeStruct((1, bands), f32),
+                   jax.ShapeDtypeStruct((1, bands), f32)),
+        in_specs=[anywhere, vmem],
+        out_specs=(hbm, hbm, hbm),
+        scratch_shapes=[pltpu.VMEM((1, bands), f32)] * 2 + [pltpu.SemaphoreType.DMA((3,))],
+        compiler_params=pltpu.CompilerParams(vmem_limit_bytes=8 * 1024 * 1024),
+    )(in_vmem(applied), in_vmem(every))
+    return out.reshape(wavefunctions.shape), rayleigh.reshape(bands), residual.reshape(bands)
 
 
 def gather_kernel(size_y, size_z, own_ref, out_ref, send, recv):
@@ -597,9 +659,8 @@
     if fits:
         folding = fold_rows(length, size_z, 3 * size_z) or fold_rows(length, size_z, 2 * size_z)
     if folding is not None:
-        applied, rayleigh, residual = fused_hamiltonian(
-            wavefunctions, potential, cutoff_sq, folding, step)
-        return (applied, rayleigh, residual * unlocked)
+        return fused_hamiltonian(
+            wavefunctions, potential, cutoff_sq, locked_mask, folding, step)
     forward = make_tables(length, False)
     inverse = make_tables(length, True)
     rows = length // size_z

time: 194 us -> 181 us (0.933)
  Pallas kernels: 185 us -> 179 us
  local copies, waits for them, and re-layouts: 5.99 us -> 0.65 us
    pallas_call x1, Pallas kernels: 185 us -> 177 us  [fused_hamiltonian(): pl.pallas_call(functools.partial(main_kernel, size_y, size_z, step, first...]
    unnamed x1 -> x2, local copies, waits for them, and re-layouts: 4.8 us -> 0.65 us
    pallas_call x0 -> x1, Pallas kernels: none -> 2.05 us  [fused_hamiltonian(): pl.pallas_call(functools.partial(finish_kernel, bands), out_shape=(jax.Sh...]
where the time goes in v2:
time: 181 us
  Pallas kernels  179 us (99%)
    pallas_call x1, Pallas kernels, fused_hamiltonian(): pl.pallas_call(functools.partial(main_kernel, size_y, size_z, step, first...  177 us

profile of v2, /device:TPU:0, one launch (start us, length us, event | category | flops | bytes accessed | tf_op | source)
XLA Modules:
  0.0 181.1 jit_solution(6518262511528377299)
XLA Ops:
  1.3 0.0 copy-start
  1.3 0.6 copy-done
  1.9 177.1 %shard_map.139 = (f32[2,4,2,16,32,128]{5,4,3,2,1,0:T(8,128)S(1)}, f32[33,1,128]{2,1,0:T(1,128)S(1)}) custom-call(f32[2,4,2,16,32,128]{5,4,3,2,1,0:T(8,128)} %bitcast.4, s32[1]{0:T(128)S(6)} %copy.15.cut_ref, s32[8]{0:T(128)S(1)} %copy-done, bf16[512,256]{1,0:T(8,128)(2,1)} %constant.16.clone.xf_hbm, bf16[256,512]{1,0:T(8,128)(2,1)} %constant.20.clone.yf_hbm, ...), custom_call_target="tpu_custom_call" | custom-call | tf_op jit(solution)/shard_map/pallas_call | solution.py:542
  179.1 2.0 %shard_map.140 = (f32[2,4,2,16,32,128]{5,4,3,2,1,0:T(8,128)}, f32[1,8]{1,0:T(1,128)}, f32[1,8]{1,0:T(1,128)}) custom-call(f32[2,4,2,16,32,128]{5,4,3,2,1,0:T(8,128)S(1)} %get-tuple-element.8.applied_ref, f32[33,1,128]{2,1,0:T(1,128)S(1)} %get-tuple-element.9.every_ref), custom_call_target="tpu_custom_call" | custom-call | tf_op jit(solution)/shard_map/pallas_call | solution.py:563
Async XLA Ops:
  1.3 0.7 copy-start

commit v3 on v2

--- a/solution.py
+++ b/solution.py
@@ -138,109 +138,136 @@
 
 def main_kernel(
     size_y, size_z, step, first, plan, window,
-    u_hbm, cut_ref, locked_ref, xf_hbm, yf_hbm, mask_hbm, lf_hbm, li_hbm, sq_hbm, yi_hbm, xi_hbm, pot_hbm,
+    u_hbm, cut_ref, locked_hbm, xf_hbm, yf_hbm, mask_hbm, lf_hbm, li_hbm, sq_hbm, yi_hbm, xi_hbm, pot_hbm,
     o, every,
-    u, xf_ref, yf_ref, mask_ref, lf_ref, li_ref, sq_ref, yi_ref, xi_ref, pot_ref,
+    u, locked_ref, xf_ref, yf_ref, mask_ref, lf_ref, li_ref, sq_ref, yi_ref, xi_ref, pot_ref,
     a1, r1, a2, r2, r3, sums, own,
     s1, q1, s2, q2, s3, q3, s4, q4, iu, it, sg, qg,
 ):
     me_y, me_z = lax.axis_index("py"), lax.axis_index("pz")
     _, _, slots, rows_z, rows_y, length = u.shape
-    chunks = rows_z // step
-    units = slots * chunks
     rows_k = sq_ref.shape[1]
-    unit = 2 * step * rows_k
+    per = rows_z // step + 1
+    units = slots * per
     pitch = a2.shape[1] // size_z
-    blocks = size_z * chunks
     hosts = rows_k - first
     groups = length // size_z - rows_k
     count = size_y * size_z
     bands = size_y * slots
 
-    def load(s, c):
-        zs = pl.ds(c * step, step)
-        return pltpu.make_async_copy(u_hbm.at[:, :, s, zs], u.at[:, :, s, zs], iu.at[s, c])
+    def is_whole(i):
+        return (i >= 2) & (i < units - 2)
+
+    def place(i, whole):
+        s, c = i // per, i % per
+        big = 2 * step * rows_k
+        small = big // 2 + 4
+        if whole:
+            n = c - 2 * (1 - s)
+            return s, step * (1 - s + n), step, 2 * small * (1 - s) + big * n, big
+        n = c - (per - 2) * s
+        return (s, (per - 2) * step * s + step // 2 * n, step // 2,
+                (per - 2) * big * s + small * n, small)
+
+    def each(i, act):
+        if isinstance(i, int):
+            act(i, 2 <= i < units - 2)
+            return
+
+        @pl.when(is_whole(i))
+        def _():
+            act(i, True)
+
+        @pl.when(jnp.logical_not(is_whole(i)))
+        def _():
+            act(i, False)
+
+    def load(i, whole):
+        s, z, n, _, _ = place(i, whole)
+        zs = pl.ds(z, n)
+        return pltpu.make_async_copy(u_hbm.at[:, :, s, zs], u.at[:, :, s, zs], iu.at[i])
 
     barrier = pltpu.get_barrier_semaphore()
     for d in range(1, size_z):
         pl.semaphore_signal(barrier, inc=1, device_id={"pz": (me_z + d) % size_z}, device_id_type=MESH)
     for d in range(1, size_y):
         pl.semaphore_signal(barrier, inc=1, device_id={"py": (me_y + d) % size_y}, device_id_type=MESH)
-    pairs = ((xf_hbm, xf_ref), (yf_hbm, yf_ref), (mask_hbm, mask_ref), (lf_hbm, lf_ref), (li_hbm, li_ref),
+    pairs = ((locked_hbm, locked_ref), (xf_hbm, xf_ref), (yf_hbm, yf_ref), (mask_hbm, mask_ref), (lf_hbm, lf_ref), (li_hbm, li_ref),
              (sq_hbm, sq_ref), (yi_hbm, yi_ref), (xi_hbm, xi_ref), (pot_hbm, pot_ref))
     fetches = [pltpu.make_async_copy(src, dst, it.at[n]) for n, (src, dst) in enumerate(pairs)]
-    fetches[0].start()
-    load(0, 0).start()
-    for fetch in fetches[1:]:
-        fetch.start()
-    for i in range(1, units):
-        load(i // chunks, i % chunks).start()
-
-    def copy1(s, c, d):
+    fetches[1].start()
+    for i in range(2):
+        load(i, False).start()
+    for n, fetch in enumerate(fetches):
+        if n != 1:
+            fetch.start()
+    for i in range(2, units):
+        load(i, 2 <= i < units - 2).start()
+
+    def copy1(i, whole, d):
+        s, z, n, _, _ = place(i, whole)
         to = (me_y + d) % size_y
         return pltpu.make_async_remote_copy(
-            src_ref=a1.at[:, to, s, pl.ds(c * step, step)],
-            dst_ref=r1.at[:, s, pl.ds(c * step, step), me_y],
-            send_sem=s1, recv_sem=q1.at[s, c],
-            device_id={"py": to}, device_id_type=MESH)
-
-    def rows2(m, c):
-        return pl.ds(pl.multiple_of(m * pitch + c * unit, 8), unit)
-
-    def rows_r(m, c):
-        return pl.ds(pl.multiple_of((m * chunks + c) * unit, 8), unit)
-
-    def copy2(s, c, d):
+            src_ref=a1.at[:, to, s, pl.ds(z, n)], dst_ref=r1.at[:, s, pl.ds(z, n), me_y],
+            send_sem=s1, recv_sem=q1.at[i], device_id={"py": to}, device_id_type=MESH)
+
+    def rows_at(m, base, count):
+        return pl.ds(pl.multiple_of(m * pitch + base, 8), count)
+
+    def copy2(i, whole, d):
+        s, _, _, base, rows = place(i, whole)
         to = (me_z + d) % size_z
         return pltpu.make_async_remote_copy(
-            src_ref=a2.at[s, rows2(to, c)], dst_ref=r2.at[s, rows_r(me_z, c)],
-            send_sem=s2, recv_sem=q2.at[s, c],
-            device_id={"pz": to}, device_id_type=MESH)
-
-    def copy3(s, c, d):
+            src_ref=a2.at[s, rows_at(to, base, rows)], dst_ref=r2.at[s, rows_at(me_z, base, rows)],
+            send_sem=s2, recv_sem=q2.at[i], device_id={"pz": to}, device_id_type=MESH)
+
+    def copy3(i, whole, d):
+        s, _, _, base, rows = place(i, whole)
         to = (me_z + d) % size_z
         return pltpu.make_async_remote_copy(
-            src_ref=r2.at[s, rows_r(to, c)], dst_ref=r3.at[s, rows2(me_z, c)],
-            send_sem=s3, recv_sem=q3.at[s, c],
-            device_id={"pz": to}, device_id_type=MESH)
-
-    def copy4(s, c, d):
+            src_ref=r2.at[s, rows_at(to, base, rows)], dst_ref=r3.at[s, rows_at(me_z, base, rows)],
+            send_sem=s3, recv_sem=q3.at[i], device_id={"pz": to}, device_id_type=MESH)
+
+    def copy4(i, whole, d):
+        s, z, n, _, _ = place(i, whole)
         to = (me_y + d) % size_y
         return pltpu.make_async_remote_copy(
-            src_ref=r1.at[:, s, pl.ds(c * step, step), to],
-            dst_ref=o.at[:, me_y, s, pl.ds(c * step, step)],
-            send_sem=s4, recv_sem=q4.at[s, c],
-            device_id={"py": to}, device_id_type=MESH)
+            src_ref=r1.at[:, s, pl.ds(z, n), to], dst_ref=o.at[:, me_y, s, pl.ds(z, n)],
+            send_sem=s4, recv_sem=q4.at[i], device_id={"py": to}, device_id_type=MESH)
 
     order_z = sorted(range(1, size_z), key=lambda d: -min(d, size_z - d))
     order_y = sorted(range(1, size_y), key=lambda d: -min(d, size_y - d))
 
-    def forward_x(i, leave):
-        s, c = i // chunks, i % chunks
-        load(s, c).wait()
-        zs = pl.ds(c * step, step)
+    def forward_x(i, whole, leave=True):
+        s, z, n, _, _ = place(i, whole)
+        load(i, whole).wait()
+        zs = pl.ds(z, n)
         for d in order_y + [0]:
             to = (me_y + d) % size_y
             rows = jnp.concatenate(
-                [u[p, to, s, zs].reshape(step * rows_y, length) for p in range(2)], axis=1)
+                [u[p, to, s, zs].reshape(n * rows_y, length) for p in range(2)], axis=1)
             done = right_dot(rows, xf_ref)
             for p in range(2):
-                part = done[:, p * length : (p + 1) * length].reshape(step, rows_y, length)
+                part = done[:, p * length : (p + 1) * length].reshape(n, rows_y, length)
                 if d == 0:
                     r1[p, s, zs, me_y] = part
                 else:
                     a1[p, to, s, zs] = part
             if d > 0 and leave:
-                copy1(s, c, d).start()
-
-    def forward_y(i):
-        s, c = i // chunks, i % chunks
-        await_all(a1.at[:, pl.ds(0, size_y - 1), s, pl.ds(c * step, step)], q1.at[s, c])
-        for z in range(0, step, 2):
+                copy1(i, whole, d).start()
+
+    def packed(i, whole, g, p, z):
+        _, _, n, base, _ = place(i, whole)
+        return base + g * 2 * n + p * n + z
+
+    def forward_y(i, whole):
+        s, first_z, n, base, count_rows = place(i, whole)
+        await_all(a1.at[:, pl.ds(0, size_y - 1), s, pl.ds(first_z, n)], q1.at[i])
+        for z in range(0, n, 2):
             sides = []
             for e in range(2):
                 sides.append(jnp.concatenate(
-                    [r1[p, s, c * step + z + e].reshape(length, length) for p in range(2)], axis=0))
+                    [r1[p, s, first_z + z + e].reshape(length, length) for p in range(2)], axis=0))
             done = left_dot(yf_ref, jnp.concatenate(sides, axis=1))
             for p in range(2):
                 for e in range(2):
@@ -252,43 +279,48 @@
                         part[first + h] = part[first + h] + pltpu.roll(
                             part[rows_k + g], shift, axis=1) * mask_ref[t]
                     for g in range(rows_k):
-                        a2[s, pl.ds(c * unit + g * 2 * step + p * step + z + e, size_z, stride=pitch)] = part[g]
-        r2[s, rows_r(me_z, c)] = a2[s, rows2(me_z, c)]
-
-    def leave2(i):
+                        a2[s, pl.ds(packed(i, whole, g, p, z + e), size_z, stride=pitch)] = part[g]
+        r2[s, rows_at(me_z, base, count_rows)] = a2[s, rows_at(me_z, base, count_rows)]
+
+    def leave2(i, whole):
         for d in order_z:
-            copy2(i // chunks, i % chunks, d).start()
-
-    def arrive2(i):
-        await_all(a2.at[0, pl.ds(0, (size_z - 1) * unit)], q2.at[i // chunks, i % chunks])
-
-    def leave3(i):
+            copy2(i, whole, d).start()
+
+    def arrive2(i, whole):
+        await_all(a2.at[0, pl.ds(0, (size_z - 1) * place(i, whole)[4])], q2.at[i])
+
+    def leave3(i, whole):
         for d in order_z:
-            copy3(i // chunks, i % chunks, d).start()
-
-    def arrive3(i):
-        await_all(a2.at[0, pl.ds(0, (size_z - 1) * unit)], q3.at[i // chunks, i % chunks])
+            copy3(i, whole, d).start()
+
+    def arrive3(i, whole):
+        await_all(a2.at[0, pl.ds(0, (size_z - 1) * place(i, whole)[4])], q3.at[i])
 
     kz = lax.broadcasted_iota(jnp.int32, (length, length), 0)
     kz_sq = signed_square(kz, length)
 
     def z_rows(s, ks):
-        def at(k, p, i):
-            return pl.ds(k * 2 * step + p * step + i, blocks, stride=unit)
+        spots = []
+        for i in range(s * per, s * per + per):
+            whole = 2 <= i < units - 2
+            spots += [(i, whole, z) for z in range(place(i, whole)[2])]
+
+        def at(k, p, spot):
+            i, whole, z = spot
+            return pl.ds(packed(i, whole, k, p, z), size_z, stride=pitch)
         sides, weights = [], []
         for k in ks:
             sides.append(jnp.concatenate(
-                [r2[s, at(k, p, i)] for p in range(2) for i in range(step)], axis=0))
+                [r2[s, at(k, p, spot)] for p in range(2) for spot in spots], axis=0))
             weights.append(weigh(kz_sq + sq_ref[me_z, pl.ds(k, 1)], cut_ref, length))
         weight = jnp.concatenate(weights, axis=1)
         spectrum = left_dot(lf_ref, jnp.concatenate(sides, axis=1))
         done = left_dot(li_ref, spectrum * jnp.concatenate([weight, weight], axis=0))
         for e, k in enumerate(ks):
             for p in range(2):
-                for i in range(step):
-                    r2[s, at(k, p, i)] = done[
-                        p * length + i * blocks : p * length + (i + 1) * blocks,
-                        e * length : (e + 1) * length]
+                for n, spot in enumerate(spots):
+                    top = p * length + n * size_z
+                    r2[s, at(k, p, spot)] = done[top : top + size_z, e * length : (e + 1) * length]
 
     def both_z(s):
         def two_rows(h, carry):
@@ -297,20 +329,16 @@
         lax.fori_loop(0, rows_k // 2, two_rows, 0)
         if rows_k % 2:
             z_rows(s, (rows_k - 1,))
-
-        def keep(c, carry):
-            r3[s, rows2(me_z, c)] = r2[s, rows_r(me_z, c)]
-            return carry
-        lax.fori_loop(0, chunks, keep, 0)
-
-    def inverse_y(i):
-        s, c = i // chunks, i % chunks
-        for z in range(0, step, 2):
+        r3[s, rows_at(me_z, 0, pitch)] = r2[s, rows_at(me_z, 0, pitch)]
+
+    def inverse_y(i, whole):
+        s, first_z, n, _, _ = place(i, whole)
+        for z in range(0, n, 2):
             sides = []
             for e in range(2):
                 both = []
                 for p in range(2):
-                    part = [r3[s, pl.ds(c * unit + g * 2 * step + p * step + z + e, size_z, stride=pitch)]
+                    part = [r3[s, pl.ds(packed(i, whole, g, p, z + e), size_z, stride=pitch)]
                             for g in range(rows_k)]
                     guests = [None] * groups
                     for t, (h, g, shift) in enumerate(plan):
@@ -324,18 +352,18 @@
             for p in range(2):
                 for e in range(2):
                     part = done[p * length : (p + 1) * length, e * length : (e + 1) * length]
-                    r1[p, s, c * step + z + e] = part.reshape(size_y, rows_y, length)
+                    r1[p, s, first_z + z + e] = part.reshape(size_y, rows_y, length)
         for d in order_y:
-            copy4(s, c, d).start()
-        zs = pl.ds(c * step, step)
+            copy4(i, whole, d).start()
+        zs = pl.ds(first_z, n)
         o[:, me_y, s, zs] = r1[:, s, zs, me_y]
 
-    def inverse_x(i):
-        s, c = i // chunks, i % chunks
-        zs = pl.ds(c * step, step)
-        area = step * rows_y
+    def inverse_x(i, whole):
+        s, z, n, _, _ = place(i, whole)
+        zs = pl.ds(z, n)
+        area = n * rows_y
         pot = pot_ref[zs].reshape(area, length)
-        await_all(a1.at[:, pl.ds(0, size_y - 1), s, zs], q4.at[s, c])
+        await_all(a1.at[:, pl.ds(0, size_y - 1), s, zs], q4.at[i])
         for d in range(size_y):
             owner = (me_y + size_y - d) % size_y
             rows = jnp.concatenate(
@@ -345,7 +373,7 @@
             for p in range(2):
                 field = u[p, owner, s, zs].reshape(area, length)
                 part = done[:, p * length : (p + 1) * length] + pot * field
-                o[p, owner, s, zs] = part.reshape(step, rows_y, length)
+                o[p, owner, s, zs] = part.reshape(n, rows_y, length)
                 fields.append(field.reshape(area // 8, 8, length))
                 results.append(part.reshape(area // 8, 8, length))
 
@@ -357,73 +385,71 @@
             gaps = [r - shift[None] * f for f, r in zip(fields, results)]
             values = (norm, corr, shift, total([g * g for g in gaps]),
                       total([g * f for g, f in zip(gaps, fields)]))
-            for n, value in enumerate(values):
-                sums[n, owner, s, c] = value
-
-    ahead = min(2, units)
-    fetches[0].wait()
+            for k, value in enumerate(values):
+                sums[k, owner, s, i % per] = value
+
+    fetches[1].wait()
 
     def before(i, carry):
-        forward_x(i, False)
+        forward_x(i, False, False)
         return carry
-    lax.fori_loop(0, ahead, before, 0)
+    lax.fori_loop(0, 2, before, 0)
     pl.semaphore_wait(barrier, size_y + size_z - 2)
-
-    def depart(i, carry):
+    for i in range(2):
         for d in order_y:
-            copy1(i // chunks, i % chunks, d).start()
-        return carry
-    lax.fori_loop(0, ahead, depart, 0)
-    for fetch in fetches[1:]:
-        fetch.wait()
+            copy1(i, False, d).start()
+    for n, fetch in enumerate(fetches):
+        if n != 1:
+            fetch.wait()
 
     def outward(i, carry):
-        @pl.when(i + ahead < units)
-        def _():
-            forward_x(i + ahead, True)
-        forward_y(i)
+        @pl.when(i + 2 < units)
+        def _():
+            each(i + 2, forward_x)
+        each(i, forward_y)
 
         @pl.when(i >= window)
         def _():
-            arrive2(i - window)
-        leave2(i)
-
-        @pl.when((i >= window) & ((i - window) % chunks == chunks - 1))
-        def _():
-            both_z((i - window) // chunks)
+            each(i - window, arrive2)
+        each(i, leave2)
+
+        @pl.when(i == per - 1 + window)
+        def _():
+            both_z(0)
         return carry
     lax.fori_loop(0, units, outward, 0)
 
     def homeward(i, carry):
         @pl.when(i < window)
         def _():
-            arrive2(units - window + i)
+            each(units - window + i, arrive2)
 
         @pl.when(i >= window)
         def _():
-            arrive3(i - window)
+            each(i - window, arrive3)
 
         @pl.when(i < units)
         def _():
-            leave3(i)
-
-        @pl.when(i == window - 1)
-        def _():
-            both_z(slots - 1)
+            each(i, leave3)
+
+        @pl.when(i == per - 2)
+        def _():
+            both_z(1)
 
         @pl.when(i >= window)
         def _():
-            inverse_y(i - window)
-
-        @pl.when(i > window)
-        def _():
-            inverse_x(i - window - 1)
+            each(i - window, inverse_y)
+
+        @pl.when(i > window + 1)
+        def _():
+            each(i - window - 2, inverse_x)
         return carry
     lax.fori_loop(0, units + window, homeward, 0)
-    inverse_x(units - 1)
+    for i in range(units - 2, units):
+        inverse_x(i, False)
 
     norm, corr, shift, rest_sq, rest_dot = (
-        sums[n].reshape(bands, chunks * 8, length) for n in range(5))
+        sums[n].reshape(bands, per * 8, length) for n in range(5))
 
     def of_band(value):
         return jnp.sum(jnp.sum(value, axis=1), axis=1, keepdims=True)
@@ -459,7 +485,7 @@
     for sem in (s1, s4):
         await_all(a1.at[:, pl.ds(0, size_y - 1)], sem)
     for sem in (s2, s3):
-        await_all(a2.at[:, pl.ds(0, (size_z - 1) * chunks * unit)], sem)
+        await_all(a2.at[:, pl.ds(0, (size_z - 1) * pitch)], sem)
     for sem in (sg, qg):
         await_all(every.at[pl.ds(0, count - 1)], sem)
 
@@ -513,14 +539,13 @@
     size_y, size_z = lax.axis_size("py"), lax.axis_size("pz")
     slots = bands // size_y
     rows_k = square.shape[0] // size_z
-    chunks = rows_z // step
-    unit = 2 * step * rows_k
-    pitch = chunks * unit + 8
-    blocks = size_z * chunks
+    per = rows_z // step + 1
+    units = slots * per
+    pitch = 2 * rows_z * rows_k + 8
     count = size_y * size_z
     xf, xi = exact_matrix(length, False), exact_matrix(length, True)
     both_y = np.concatenate([order, order + length])
-    order_z = (step * np.arange(blocks)[None, :] + np.arange(step)[:, None]).reshape(-1)
+    order_z = (rows_z * np.arange(size_z)[None, :] + np.arange(rows_z)[:, None]).reshape(-1)
     both_z = np.concatenate([order_z, order_z + length])
     tables = [np.concatenate(two_parts(t), axis=0) for t in (xf, xi)]
     tables += [np.concatenate(two_parts(t), axis=1)
@@ -530,10 +555,10 @@
     xf_t, xi_t, lf_t, li_t, yf_t, yi_t = tables
     field = wavefunctions.reshape(2, size_y, slots, rows_z, rows_y, length)
     vmem = pl.BlockSpec(memory_space=pltpu.VMEM)
-    smem = pl.BlockSpec(memory_space=pltpu.SMEM)
     anywhere = pl.BlockSpec(memory_space=pl.ANY)
     hbm = pl.BlockSpec(memory_space=pltpu.HBM)
-    here = pltpu.SemaphoreType.DMA((slots, chunks))
+    smem = pl.BlockSpec(memory_space=pltpu.SMEM)
+    here = pltpu.SemaphoreType.DMA((units,))
     once = pltpu.SemaphoreType.DMA
     f32 = jnp.float32
     in_hbm = functools.partial(pltpu.with_memory_space_constraint, memory_space=pltpu.HBM)
@@ -542,24 +567,24 @@
     applied, every = pl.pallas_call(
         functools.partial(main_kernel, size_y, size_z, step, first, plan, WINDOW),
         out_shape=(pltpu.VMEM(field.shape, f32), pltpu.VMEM((count + 1, 1, length), f32)),
-        in_specs=[hbm, smem, smem] + [hbm] * len(operands),
+        in_specs=[hbm, smem] + [hbm] * (len(operands) + 1),
         out_specs=(vmem, vmem),
-        scratch_shapes=[pltpu.VMEM(field.shape, f32)]
+        scratch_shapes=[pltpu.VMEM(field.shape, f32), pltpu.SMEM((bands,), jnp.int32)]
         + [pltpu.VMEM(x.shape, x.dtype) for x in operands]
         + [
             pltpu.VMEM(field.shape, f32),
             pltpu.VMEM((2, slots, rows_z, size_y, rows_y, length), f32),
             pltpu.VMEM((slots, size_z * pitch, length), f32),
-            pltpu.VMEM((slots, blocks * unit, length), f32),
             pltpu.VMEM((slots, size_z * pitch, length), f32),
-            pltpu.VMEM((5, size_y, slots, chunks, 8, length), f32),
+            pltpu.VMEM((slots, size_z * pitch, length), f32),
+            pltpu.VMEM((5, size_y, slots, per, 8, length), f32),
             pltpu.VMEM((1, length), f32),
             once, here, once, here, once, here, once, here, here,
-            pltpu.SemaphoreType.DMA((len(operands),)), once, once,
+            pltpu.SemaphoreType.DMA((len(operands) + 1,)), once, once,
         ],
         compiler_params=pltpu.CompilerParams(
             collective_id=0, has_side_effects=True, vmem_limit_bytes=48 * 1024 * 1024),
-    )(in_hbm(field), cutoff_sq, locked_mask, *[in_hbm(x) for x in operands])
+    )(in_hbm(field), cutoff_sq, *[in_hbm(x) for x in (locked_mask,) + operands])
     out, rayleigh, residual = pl.pallas_call(
         functools.partial(finish_kernel, bands),
         out_shape=(jax.ShapeDtypeStruct(field.shape, f32), jax.ShapeDtypeStruct((1, bands), f32),
@@ -653,8 +678,9 @@
     size_y, size_z = lax.axis_size("py"), lax.axis_size("pz")
     step = 4
     unlocked = 1.0 - locked_mask.astype(jnp.float32)
-    fits = size_z == 8 and bands == 8 and length % 128 == 0 and bands % size_y == 0
-    fits = fits and rows_z % step == 0 and step * rows_y % 8 == 0
+    fits = size_z == 8 and bands == 8 and length % 128 == 0
+    fits = fits and rows_z % step == 0 and rows_z > step and rows_y % 8 == 0
+    fits = fits and bands == 2 * size_y
     folding = None
     if fits:
         folding = fold_rows(length, size_z, 3 * size_z) or fold_rows(length, size_z, 2 * size_z)

time: 181 us -> 178 us (0.983)
  Pallas kernels: 179 us -> 176 us
    pallas_call x1, Pallas kernels: 177 us -> 174 us  [fused_hamiltonian(): pl.pallas_call(functools.partial(main_kernel, size_y, size_z, step, first...]
where the time goes in v3:
time: 178 us
  Pallas kernels  176 us (99%)
    pallas_call x1, Pallas kernels, fused_hamiltonian(): pl.pallas_call(functools.partial(main_kernel, size_y, size_z, step, first...  174 us

profile of v3, /device:TPU:0, one launch (start us, length us, event | category | flops | bytes accessed | tf_op | source)
XLA Modules:
  0.0 177.6 jit_solution(12841785090663767280)
XLA Ops:
  1.3 174.2 %shard_map.139 = (f32[2,4,2,16,32,128]{5,4,3,2,1,0:T(8,128)S(1)}, f32[33,1,128]{2,1,0:T(1,128)S(1)}) custom-call(f32[2,4,2,16,32,128]{5,4,3,2,1,0:T(8,128)} %bitcast.4, s32[1]{0:T(128)S(6)} %copy.15.cut_ref, s32[8]{0:T(128)} %locked_hbm.1, bf16[512,256]{1,0:T(8,128)(2,1)} %constant.16.clone.xf_hbm, bf16[256,512]{1,0:T(8,128)(2,1)} %constant.20.clone.yf_hbm, ...), custom_call_target="tpu_custom_call" | custom-call | tf_op jit(solution)/shard_map/pallas_call | solution.py:567
  175.5 2.0 %shard_map.140 = (f32[2,4,2,16,32,128]{5,4,3,2,1,0:T(8,128)}, f32[1,8]{1,0:T(1,128)}, f32[1,8]{1,0:T(1,128)}) custom-call(f32[2,4,2,16,32,128]{5,4,3,2,1,0:T(8,128)S(1)} %get-tuple-element.8.applied_ref, f32[33,1,128]{2,1,0:T(1,128)S(1)} %get-tuple-element.9.every_ref), custom_call_target="tpu_custom_call" | custom-call | tf_op jit(solution)/shard_map/pallas_call | solution.py:588

commit v4 on v3

--- a/solution.py
+++ b/solution.py
@@ -141,49 +141,50 @@
     u_hbm, cut_ref, locked_hbm, xf_hbm, yf_hbm, mask_hbm, lf_hbm, li_hbm, sq_hbm, yi_hbm, xi_hbm, pot_hbm,
     o, every,
     u, locked_ref, xf_ref, yf_ref, mask_ref, lf_ref, li_ref, sq_ref, yi_ref, xi_ref, pot_ref,
-    a1, r1, a2, r2, r3, sums, own,
+    a1, r1, a2, r2, r3, r4, sums, own,
     s1, q1, s2, q2, s3, q3, s4, q4, iu, it, sg, qg,
 ):
     me_y, me_z = lax.axis_index("py"), lax.axis_index("pz")
     _, _, slots, rows_z, rows_y, length = u.shape
     rows_k = sq_ref.shape[1]
-    per = rows_z // step + 1
-    units = slots * per
+    chunks = rows_z // step
+    units = slots * chunks + 1
     pitch = a2.shape[1] // size_z
+    big = 2 * step * rows_k
+    small = big // 2 + 4
     hosts = rows_k - first
     groups = length // size_z - rows_k
     count = size_y * size_z
     bands = size_y * slots
 
-    def is_whole(i):
-        return (i >= 2) & (i < units - 2)
-
-    def place(i, whole):
-        s, c = i // per, i % per
-        big = 2 * step * rows_k
-        small = big // 2 + 4
+    def is_whole(i, back):
+        return i < units - 2 if back else i >= 2
+
+    def place(i, whole, back):
         if whole:
-            n = c - 2 * (1 - s)
-            return s, step * (1 - s + n), step, 2 * small * (1 - s) + big * n, big
-        n = c - (per - 2) * s
-        return (s, (per - 2) * step * s + step // 2 * n, step // 2,
-                (per - 2) * big * s + small * n, small)
-
-    def each(i, act):
+            n = i if back else i - 1
+            s, c = n // chunks, n % chunks
+            return s, step * c, step, big * c + (0 if back else 8 * (1 - s)), big
+        if back:
+            n, c = i - (units - 2), chunks - 1
+            return slots - 1, step * c + step // 2 * n, step // 2, big * c + small * n, small
+        return 0, step // 2 * i, step // 2, small * i, small
+
+    def each(i, act, back):
         if isinstance(i, int):
-            act(i, 2 <= i < units - 2)
+            act(i, is_whole(i, back))
             return
 
-        @pl.when(is_whole(i))
+        @pl.when(is_whole(i, back))
         def _():
             act(i, True)
 
-        @pl.when(jnp.logical_not(is_whole(i)))
+        @pl.when(jnp.logical_not(is_whole(i, back)))
         def _():
             act(i, False)
 
     def load(i, whole):
-        s, z, n, _, _ = place(i, whole)
+        s, z, n, _, _ = place(i, whole, False)
         zs = pl.ds(z, n)
         return pltpu.make_async_copy(u_hbm.at[:, :, s, zs], u.at[:, :, s, zs], iu.at[i])
 
@@ -202,10 +203,10 @@
         if n != 1:
             fetch.start()
     for i in range(2, units):
-        load(i, 2 <= i < units - 2).start()
+        load(i, True).start()
 
     def copy1(i, whole, d):
-        s, z, n, _, _ = place(i, whole)
+        s, z, n, _, _ = place(i, whole, False)
         to = (me_y + d) % size_y
         return pltpu.make_async_remote_copy(
             src_ref=a1.at[:, to, s, pl.ds(z, n)], dst_ref=r1.at[:, s, pl.ds(z, n), me_y],
@@ -215,21 +216,21 @@
         return pl.ds(pl.multiple_of(m * pitch + base, 8), count)
 
     def copy2(i, whole, d):
-        s, _, _, base, rows = place(i, whole)
+        s, _, _, base, rows = place(i, whole, False)
         to = (me_z + d) % size_z
         return pltpu.make_async_remote_copy(
             src_ref=a2.at[s, rows_at(to, base, rows)], dst_ref=r2.at[s, rows_at(me_z, base, rows)],
-            send_sem=s2, recv_sem=q2.at[i], device_id={"pz": to}, device_id_type=MESH)
+            send_sem=s2.at[s], recv_sem=q2.at[i], device_id={"pz": to}, device_id_type=MESH)
 
     def copy3(i, whole, d):
-        s, _, _, base, rows = place(i, whole)
+        s, _, _, base, rows = place(i, whole, True)
         to = (me_z + d) % size_z
         return pltpu.make_async_remote_copy(
-            src_ref=r2.at[s, rows_at(to, base, rows)], dst_ref=r3.at[s, rows_at(me_z, base, rows)],
-            send_sem=s3, recv_sem=q3.at[i], device_id={"pz": to}, device_id_type=MESH)
+            src_ref=r4.at[s, rows_at(to, base, rows)], dst_ref=r3.at[s, rows_at(me_z, base, rows)],
+            send_sem=s3.at[s], recv_sem=q3.at[i], device_id={"pz": to}, device_id_type=MESH)
 
     def copy4(i, whole, d):
-        s, z, n, _, _ = place(i, whole)
+        s, z, n, _, _ = place(i, whole, True)
         to = (me_y + d) % size_y
         return pltpu.make_async_remote_copy(
             src_ref=r1.at[:, s, pl.ds(z, n), to], dst_ref=o.at[:, me_y, s, pl.ds(z, n)],
@@ -239,7 +240,7 @@
     order_y = sorted(range(1, size_y), key=lambda d: -min(d, size_y - d))
 
     def forward_x(i, whole, leave=True):
-        s, z, n, _, _ = place(i, whole)
+        s, z, n, _, _ = place(i, whole, False)
         load(i, whole).wait()
         zs = pl.ds(z, n)
         for d in order_y + [0]:
@@ -256,12 +257,12 @@
             if d > 0 and leave:
                 copy1(i, whole, d).start()
 
-    def packed(i, whole, g, p, z):
-        _, _, n, base, _ = place(i, whole)
+    def packed(i, whole, back, g, p, z):
+        _, _, n, base, _ = place(i, whole, back)
         return base + g * 2 * n + p * n + z
 
     def forward_y(i, whole):
-        s, first_z, n, base, count_rows = place(i, whole)
+        s, first_z, n, base, count_rows = place(i, whole, False)
         await_all(a1.at[:, pl.ds(0, size_y - 1), s, pl.ds(first_z, n)], q1.at[i])
         for z in range(0, n, 2):
             sides = []
@@ -279,7 +280,7 @@
                         part[first + h] = part[first + h] + pltpu.roll(
                             part[rows_k + g], shift, axis=1) * mask_ref[t]
                     for g in range(rows_k):
-                        a2[s, pl.ds(packed(i, whole, g, p, z + e), size_z, stride=pitch)] = part[g]
+                        a2[s, pl.ds(packed(i, whole, False, g, p, z + e), size_z, stride=pitch)] = part[g]
         r2[s, rows_at(me_z, base, count_rows)] = a2[s, rows_at(me_z, base, count_rows)]
 
     def leave2(i, whole):
@@ -287,40 +288,42 @@
             copy2(i, whole, d).start()
 
     def arrive2(i, whole):
-        await_all(a2.at[0, pl.ds(0, (size_z - 1) * place(i, whole)[4])], q2.at[i])
+        await_all(a2.at[0, pl.ds(0, (size_z - 1) * place(i, whole, False)[4])], q2.at[i])
 
     def leave3(i, whole):
         for d in order_z:
             copy3(i, whole, d).start()
 
     def arrive3(i, whole):
-        await_all(a2.at[0, pl.ds(0, (size_z - 1) * place(i, whole)[4])], q3.at[i])
+        await_all(a2.at[0, pl.ds(0, (size_z - 1) * place(i, whole, True)[4])], q3.at[i])
 
     kz = lax.broadcasted_iota(jnp.int32, (length, length), 0)
     kz_sq = signed_square(kz, length)
 
     def z_rows(s, ks):
-        spots = []
-        for i in range(s * per, s * per + per):
-            whole = 2 <= i < units - 2
-            spots += [(i, whole, z) for z in range(place(i, whole)[2])]
-
-        def at(k, p, spot):
-            i, whole, z = spot
-            return pl.ds(packed(i, whole, k, p, z), size_z, stride=pitch)
+        spots = [[], []]
+        for back in range(2):
+            for i in range(units):
+                whole = is_whole(i, back)
+                if place(i, whole, back)[0] == s:
+                    spots[back] += [(i, whole, z) for z in range(place(i, whole, back)[2])]
+
+        def at(k, p, n, back):
+            i, whole, z = spots[back][n]
+            return pl.ds(packed(i, whole, back, k, p, z), size_z, stride=pitch)
         sides, weights = [], []
         for k in ks:
             sides.append(jnp.concatenate(
-                [r2[s, at(k, p, spot)] for p in range(2) for spot in spots], axis=0))
+                [r2[s, at(k, p, n, 0)] for p in range(2) for n in range(rows_z)], axis=0))
             weights.append(weigh(kz_sq + sq_ref[me_z, pl.ds(k, 1)], cut_ref, length))
         weight = jnp.concatenate(weights, axis=1)
         spectrum = left_dot(lf_ref, jnp.concatenate(sides, axis=1))
         done = left_dot(li_ref, spectrum * jnp.concatenate([weight, weight], axis=0))
         for e, k in enumerate(ks):
             for p in range(2):
-                for n, spot in enumerate(spots):
+                for n in range(rows_z):
                     top = p * length + n * size_z
-                    r2[s, at(k, p, spot)] = done[top : top + size_z, e * length : (e + 1) * length]
+                    r4[s, at(k, p, n, 1)] = done[top : top + size_z, e * length : (e + 1) * length]
 
     def both_z(s):
         def two_rows(h, carry):
@@ -329,16 +332,16 @@
         lax.fori_loop(0, rows_k // 2, two_rows, 0)
         if rows_k % 2:
             z_rows(s, (rows_k - 1,))
-        r3[s, rows_at(me_z, 0, pitch)] = r2[s, rows_at(me_z, 0, pitch)]
+        r3[s, rows_at(me_z, 0, pitch)] = r4[s, rows_at(me_z, 0, pitch)]
 
     def inverse_y(i, whole):
-        s, first_z, n, _, _ = place(i, whole)
+        s, first_z, n, _, _ = place(i, whole, True)
         for z in range(0, n, 2):
             sides = []
             for e in range(2):
                 both = []
                 for p in range(2):
-                    part = [r3[s, pl.ds(packed(i, whole, g, p, z + e), size_z, stride=pitch)]
+                    part = [r3[s, pl.ds(packed(i, whole, True, g, p, z + e), size_z, stride=pitch)]
                             for g in range(rows_k)]
                     guests = [None] * groups
                     for t, (h, g, shift) in enumerate(plan):
@@ -359,7 +362,7 @@
         o[:, me_y, s, zs] = r1[:, s, zs, me_y]
 
     def inverse_x(i, whole):
-        s, z, n, _, _ = place(i, whole)
+        s, z, n, _, _ = place(i, whole, True)
         zs = pl.ds(z, n)
         area = n * rows_y
         pot = pot_ref[zs].reshape(area, length)
@@ -386,8 +389,9 @@
             values = (norm, corr, shift, total([g * g for g in gaps]),
                       total([g * f for g, f in zip(gaps, fields)]))
             for k, value in enumerate(values):
-                sums[k, owner, s, i % per] = value
-
+                sums[k, owner, s, z // step if whole else z // (step // 2) - (chunks - 1)] = value
+
+    sums[:, :, :, chunks] = jnp.zeros((5, size_y, slots, 8, length), jnp.float32)
     fetches[1].wait()
 
     def before(i, carry):
@@ -405,15 +409,15 @@
     def outward(i, carry):
         @pl.when(i + 2 < units)
         def _():
-            each(i + 2, forward_x)
-        each(i, forward_y)
+            each(i + 2, forward_x, False)
+        each(i, forward_y, False)
 
         @pl.when(i >= window)
         def _():
-            each(i - window, arrive2)
-        each(i, leave2)
-
-        @pl.when(i == per - 1 + window)
+            each(i - window, arrive2, False)
+        each(i, leave2, False)
+
+        @pl.when(i == chunks + window)
         def _():
             both_z(0)
         return carry
@@ -422,34 +426,34 @@
     def homeward(i, carry):
         @pl.when(i < window)
         def _():
-            each(units - window + i, arrive2)
+            each(units - window + i, arrive2, False)
 
         @pl.when(i >= window)
         def _():
-            each(i - window, arrive3)
+            each(i - window, arrive3, True)
 
         @pl.when(i < units)
         def _():
-            each(i, leave3)
-
-        @pl.when(i == per - 2)
+            each(i, leave3, True)
+
+        @pl.when(i == window - 1)
         def _():
             both_z(1)
 
         @pl.when(i >= window)
         def _():
-            each(i - window, inverse_y)
+            each(i - window, inverse_y, True)
 
         @pl.when(i > window + 1)
         def _():
-            each(i - window - 2, inverse_x)
+            each(i - window - 2, inverse_x, True)
         return carry
     lax.fori_loop(0, units + window, homeward, 0)
     for i in range(units - 2, units):
         inverse_x(i, False)
 
     norm, corr, shift, rest_sq, rest_dot = (
-        sums[n].reshape(bands, per * 8, length) for n in range(5))
+        sums[n].reshape(bands, (chunks + 1) * 8, length) for n in range(5))
 
     def of_band(value):
         return jnp.sum(jnp.sum(value, axis=1), axis=1, keepdims=True)
@@ -484,8 +488,9 @@
     every[count] = free
     for sem in (s1, s4):
         await_all(a1.at[:, pl.ds(0, size_y - 1)], sem)
-    for sem in (s2, s3):
-        await_all(a2.at[:, pl.ds(0, (size_z - 1) * pitch)], sem)
+    for s in range(slots):
+        for sem, extra in ((s2, 8 * (s == 0)), (s3, 8 * (s == slots - 1))):
+            await_all(a2.at[0, pl.ds(0, (size_z - 1) * (chunks * big + extra))], sem.at[s])
     for sem in (sg, qg):
         await_all(every.at[pl.ds(0, count - 1)], sem)
 
@@ -539,8 +544,8 @@
     size_y, size_z = lax.axis_size("py"), lax.axis_size("pz")
     slots = bands // size_y
     rows_k = square.shape[0] // size_z
-    per = rows_z // step + 1
-    units = slots * per
+    chunks = rows_z // step
+    units = slots * chunks + 1
     pitch = 2 * rows_z * rows_k + 8
     count = size_y * size_z
     xf, xi = exact_matrix(length, False), exact_matrix(length, True)
@@ -560,6 +565,7 @@
     smem = pl.BlockSpec(memory_space=pltpu.SMEM)
     here = pltpu.SemaphoreType.DMA((units,))
     once = pltpu.SemaphoreType.DMA
+    both = pltpu.SemaphoreType.DMA((slots,))
     f32 = jnp.float32
     in_hbm = functools.partial(pltpu.with_memory_space_constraint, memory_space=pltpu.HBM)
     in_vmem = functools.partial(pltpu.with_memory_space_constraint, memory_space=pltpu.VMEM)
@@ -577,9 +583,10 @@
             pltpu.VMEM((slots, size_z * pitch, length), f32),
             pltpu.VMEM((slots, size_z * pitch, length), f32),
             pltpu.VMEM((slots, size_z * pitch, length), f32),
-            pltpu.VMEM((5, size_y, slots, per, 8, length), f32),
+            pltpu.VMEM((slots, size_z * pitch, length), f32),
+            pltpu.VMEM((5, size_y, slots, chunks + 1, 8, length), f32),
             pltpu.VMEM((1, length), f32),
-            once, here, once, here, once, here, once, here, here,
+            once, here, both, here, both, here, once, here, here,
             pltpu.SemaphoreType.DMA((len(operands) + 1,)), once, once,
         ],
         compiler_params=pltpu.CompilerParams(

time: 178 us -> 176 us (0.989)
  no operation moved by 1% of the time
where the time goes in v4:
time: 176 us
  Pallas kernels  175 us (99%)
    pallas_call x1, Pallas kernels, fused_hamiltonian(): pl.pallas_call(functools.partial(main_kernel, size_y, size_z, step, first...  173 us

profile of v4, /device:TPU:0, one launch (start us, length us, event | category | flops | bytes accessed | tf_op | source)
XLA Modules:
  0.0 176.1 jit_solution(16201472671348024573)
XLA Ops:
  1.3 172.7 %shard_map.139 = (f32[2,4,2,16,32,128]{5,4,3,2,1,0:T(8,128)S(1)}, f32[33,1,128]{2,1,0:T(1,128)S(1)}) custom-call(f32[2,4,2,16,32,128]{5,4,3,2,1,0:T(8,128)} %bitcast.4, s32[1]{0:T(128)S(6)} %copy.15.cut_ref, s32[8]{0:T(128)} %locked_hbm.1, bf16[512,256]{1,0:T(8,128)(2,1)} %constant.16.clone.xf_hbm, bf16[256,512]{1,0:T(8,128)(2,1)} %constant.20.clone.yf_hbm, ...), custom_call_target="tpu_custom_call" | custom-call | tf_op jit(solution)/shard_map/pallas_call | solution.py:573
  174.0 2.0 %shard_map.140 = (f32[2,4,2,16,32,128]{5,4,3,2,1,0:T(8,128)}, f32[1,8]{1,0:T(1,128)}, f32[1,8]{1,0:T(1,128)}) custom-call(f32[2,4,2,16,32,128]{5,4,3,2,1,0:T(8,128)S(1)} %get-tuple-element.8.applied_ref, f32[33,1,128]{2,1,0:T(1,128)S(1)} %get-tuple-element.9.every_ref), custom_call_target="tpu_custom_call" | custom-call | tf_op jit(solution)/shard_map/pallas_call | solution.py:595

commit v5 on v4

--- a/solution.py
+++ b/solution.py
@@ -470,16 +470,15 @@
     own[...] = jnp.sum(packed, axis=0, keepdims=True)
     me = me_y * size_z + me_z
 
-    def tell(t):
-        to = (me + t) % count
+    def tell(y, z):
         return pltpu.make_async_remote_copy(
             src_ref=own, dst_ref=every.at[me], send_sem=sg, recv_sem=qg,
-            device_id={"py": to // size_z, "pz": to % size_z}, device_id_type=MESH)
-
-    def tell_start(t, carry):
-        tell(t).start()
-        return carry
-    lax.fori_loop(1, count, tell_start, 0)
+            device_id={"py": (me_y + y) % size_y, "pz": (me_z + z) % size_z}, device_id_type=MESH)
+
+    for z in order_z + [0]:
+        for y in range(size_y):
+            if y or z:
+                tell(y, z).start()
     every[me] = own[...]
     free = jnp.zeros((1, length), jnp.float32)
 

time: 176 us -> 176 us (level)
  no operation moved by 1% of the time
where the time goes in v5:
time: 176 us
  Pallas kernels  175 us (99%)
    pallas_call x1, Pallas kernels, fused_hamiltonian(): pl.pallas_call(functools.partial(main_kernel, size_y, size_z, step, first...  173 us

profile of v5, /device:TPU:0, one launch (start us, length us, event | category | flops | bytes accessed | tf_op | source)
XLA Modules:
  0.0 176.1 jit_solution(15970003969488944186)
XLA Ops:
  1.3 172.7 %shard_map.139 = (f32[2,4,2,16,32,128]{5,4,3,2,1,0:T(8,128)S(1)}, f32[33,1,128]{2,1,0:T(1,128)S(1)}) custom-call(f32[2,4,2,16,32,128]{5,4,3,2,1,0:T(8,128)} %bitcast.4, s32[1]{0:T(128)S(6)} %copy.15.cut_ref, s32[8]{0:T(128)} %locked_hbm.1, bf16[512,256]{1,0:T(8,128)(2,1)} %constant.16.clone.xf_hbm, bf16[256,512]{1,0:T(8,128)(2,1)} %constant.20.clone.yf_hbm, ...), custom_call_target="tpu_custom_call" | custom-call | tf_op jit(solution)/shard_map/pallas_call | solution.py:572
  174.0 2.0 %shard_map.140 = (f32[2,4,2,16,32,128]{5,4,3,2,1,0:T(8,128)}, f32[1,8]{1,0:T(1,128)}, f32[1,8]{1,0:T(1,128)}) custom-call(f32[2,4,2,16,32,128]{5,4,3,2,1,0:T(8,128)S(1)} %get-tuple-element.8.applied_ref, f32[33,1,128]{2,1,0:T(1,128)S(1)} %get-tuple-element.9.every_ref), custom_call_target="tpu_custom_call" | custom-call | tf_op jit(solution)/shard_map/pallas_call | solution.py:594
